TPU v7x, 32 devices: a whole 2x2x4 slice. The times are simulated.
32 devices in a mesh: gx: 16 (over z, y, x), gy: 2 (over core).
Axes of the slice: x: 2, y: 2, z: 4, core: 2. Of those that a mesh axis runs over, the one named last changes fastest.
Arguments:
- sources: bfloat16 [2048, 8, 128], P(('gx', 'gy')), may hold values from -6 to 6
- owners: int32 [2048, 1], P(('gx', 'gy')), may hold values from 0 to 15; in each aligned block of 64 rows (0 to 63, 64 to 127, ...) at most 8 rows name the same one
- strip_rows: int32 [2048], P(('gx', 'gy')), may hold values from 0 to 255
- panel_counts: int32 [2048], P(('gx', 'gy')), may hold values from 1 to 128
- arrival_bins: int32 [4096, 4, 128], P('gx'), may hold values from 0 to 254
- arrival_fracs: float32 [4096, 4, 128], P('gx'), may hold values from 0 to 1
- gain_table: bfloat16 [4096, 8, 4, 1024], P('gx'), may hold values from -0.125 to 0.125
Outputs:
- signals: float32 [1024, 4, 256], P(('gx', 'gy'))
Inputs may be any that keep to these rules, and one draw needn't show every extreme that they name: `owners`: among the rows of one device, at most 8 strips name one patch, a bound that some block reaches.
All inputs are finite; a program needn't handle non-finite values.
Results may differ from a plain program's by a relative error of at most 0.0044.
Values may be sent and summed in bfloat16 or wider, within the bound.
No kernel may reach another device: no remote copies, remote signals or barrier semaphores. Data moves between devices by JAX's collectives and lax.ppermute only.
A program may use at most 768 MiB of HBM per device.

v0:
```python
import jax
import jax.numpy as jnp
from jax import lax
from jax.sharding import PartitionSpec as P

NBIN = 256


def interp_weights(bin_ids, fractions):
    positions = jnp.arange(NBIN, dtype=jnp.int32)
    lower = jnp.where(
        positions[None, None, :] == bin_ids[:, :, None], 1.0 - fractions[:, :, None], 0.0
    )
    upper = jnp.where(
        positions[None, None, :] == bin_ids[:, :, None] + 1, fractions[:, :, None], 0.0
    )
    return (lower + upper).astype(jnp.bfloat16)


def bin_rows(row_rounded, bin_ids, fractions):
    blocks = bin_ids.shape[1]
    binned = []
    for block_index in range(blocks):
        weights = interp_weights(bin_ids[:, block_index, :], fractions[:, block_index, :])
        binned.append(
            jnp.einsum("rkp,rpb->rkb", row_rounded, weights, preferred_element_type=jnp.float32)
        )
    row_count, terms = (row_rounded.shape[0], row_rounded.shape[1])
    return jnp.stack(binned, axis=2).reshape(row_count * terms, blocks, NBIN).astype(jnp.bfloat16)


def on_device(sources, owners, strip_rows, panel_counts, arrival_bins, arrival_fracs, gain_table):
    strip_count, terms, panels = sources.shape
    shards = lax.axis_size("gx")
    columns = lax.axis_size("gy")
    capacity = 2 * strip_count // shards
    live_mask = (jnp.arange(panels, dtype=jnp.int32)[None, :] < panel_counts[:, None]).astype(
        jnp.bfloat16
    )
    masked = (sources * live_mask[:, None, :]).reshape(strip_count, terms * panels)
    targets = owners[:, 0]
    target_hot = (targets[:, None] == jnp.arange(shards, dtype=jnp.int32)[None, :]).astype(
        jnp.int32
    )
    order_in = jnp.sum((jnp.cumsum(target_hot, axis=0) - 1) * target_hot, axis=1)
    slot_of = targets * capacity + order_in
    placing = jnp.arange(shards * capacity, dtype=jnp.int32)[:, None] == slot_of[None, :]
    send_sources = jnp.dot(
        placing.astype(jnp.bfloat16), masked, preferred_element_type=jnp.float32
    ).astype(jnp.bfloat16)
    send_rows = jnp.sum(placing.astype(jnp.int32) * (strip_rows + 1)[None, :], axis=1) - 1
    got_sources, got_rows = (
        lax.all_to_all(send_sources, "gx", split_axis=0, concat_axis=0, tiled=True),
        lax.all_to_all(send_rows, "gx", split_axis=0, concat_axis=0, tiled=True),
    )
    rows_here = arrival_bins.shape[0]
    row_hot = (jnp.arange(rows_here, dtype=jnp.int32)[:, None] == got_rows[None, :]).astype(
        jnp.bfloat16
    )
    row_sources = jnp.dot(row_hot, got_sources, preferred_element_type=jnp.float32)
    blocks = arrival_bins.shape[1]
    observers = gain_table.shape[3]
    share = lax.psum_scatter(row_sources, "gy", scatter_dimension=0, tiled=True)
    share_rows = rows_here // columns
    first = lax.axis_index("gy") * share_rows
    row_rounded = share.astype(jnp.bfloat16).reshape(share_rows, terms, panels)
    own_bins = lax.dynamic_slice_in_dim(arrival_bins, first, share_rows, 0)
    own_fracs = lax.dynamic_slice_in_dim(arrival_fracs, first, share_rows, 0)
    arrived = bin_rows(row_rounded, own_bins, own_fracs)
    own_gains = lax.dynamic_slice_in_dim(gain_table, first, share_rows, 0).reshape(
        share_rows * terms, blocks, observers
    )
    return lax.psum_scatter(
        jnp.einsum("cot,cob->tob", own_gains, arrived, preferred_element_type=jnp.float32),
        ("gx", "gy"),
        scatter_dimension=0,
        tiled=True,
    )


def solution(mesh):
    placed = (
        P(("gx", "gy"), None, None),
        P(("gx", "gy"), None),
        P(("gx", "gy")),
        P(("gx", "gy")),
        P("gx", None, None),
        P("gx", None, None),
        P("gx", None, None, None),
    )
    return jax.shard_map(
        on_device,
        mesh=mesh,
        in_specs=placed,
        out_specs=P(("gx", "gy"), None, None),
        check_vma=False,
    )
```

profile of v0, /device:TPU:0, one launch (start us, length us, event | category | flops | bytes accessed | tf_op | source)
XLA Modules:
  0.0 274.6 jit_solution(13777596855906094471)
XLA Ops:
  6.5 0.7 fusion.31
  7.3 0.1 reduce_window_sum.11
  7.4 0.8 select_reduce_fusion.1
  8.2 0.7 multiply_add_fusion
  8.9 0.1 select_reduce_fusion
  9.0 0.7 sub.44
  9.7 8.3 %all-to-all-start = ((s32[16,8,1]{1,2,0:T(1,128)}), s32[16,8,1]{1,2,0:T(1,128)S(1)}, u32[]{:S(2)}, u32[]{:S(2)}) async-start(s32[16,8,1]{1,2,0:T(1,128)} %bitcast.1), calls=%async_computation | async-start | bytes 16384 | tf_op jit(solution)/shard_map/all_to_all | solution.py:54
  18.0 0.7 fusion.32
  18.8 0.9 broadcast_multiply_fusion
  19.7 1.0 fusion.25
  20.7 4.5 %all-to-all-done = s32[16,8,1]{1,2,0:T(1,128)S(1)} async-done(((s32[16,8,1]{1,2,0:T(1,128)}), s32[16,8,1]{1,2,0:T(1,128)S(1)}, u32[]{:S(2)}, u32[]{:S(2)}) %all-to-all-start) | async-done | bytes 544 | tf_op jit(solution)/shard_map/all_to_all | solution.py:54
  25.3 3.5 %all-to-all-start.1 = ((bf16[16,8,1024]{2,1,0:T(8,128)(2,1)}), bf16[16,8,1024]{2,1,0:T(8,128)(2,1)S(1)}, u32[]{:S(2)}, u32[]{:S(2)}) async-start(bf16[16,8,1024]{2,1,0:T(8,128)(2,1)} %fusion.25), calls=%async_computation.1 | async-start | bytes 524288 | tf_op jit(solution)/shard_map/all_to_all | solution.py:53
  28.9 1.5 constant_dynamic-slice_fusion.4
  30.4 1.7 constant_dynamic-slice_fusion.3
  32.1 0.5 broadcast.102
  32.6 0.7 reduce.3
  33.4 3.9 %all-to-all-done.1 = bf16[16,8,1024]{2,1,0:T(8,128)(2,1)S(1)} async-done(((bf16[16,8,1024]{2,1,0:T(8,128)(2,1)}), bf16[16,8,1024]{2,1,0:T(8,128)(2,1)S(1)}, u32[]{:S(2)}, u32[]{:S(2)}) %all-to-all-start.1) | async-done | bytes 262176 | tf_op jit(solution)/shard_map/all_to_all | solution.py:53
  37.3 1.4 fusion.26
  38.8 8.4 %constant_dynamic-slice_fusion.5 = bf16[128,8,4,1024]{3,2,1,0:T(4,128)(2,1)} fusion(bf16[256,8,4,1024]{3,2,1,0:T(4,128)(2,1)} %param.13, s32[]{:T(128)S(6)} %select_n.30), kind=kLoop, calls=%fused_computation.66 | loop fusion | bytes 16777220 | tf_op jit(solution)/shard_map/dynamic_slice | solution.py:70
  47.2 1.1 convert_bitcast_fusion
  48.3 14.7 %fusion.21 = bf16[1024,1,256]{2,0,1:T(8,128)(2,1)S(1)} fusion(bf16[128,8,128]{2,1,0:T(8,128)(2,1)S(1)} %bitcast.58, f32[128,128]{1,0:T(8,128)S(1)} %bitcast.77, s32[128,128]{1,0:T(8,128)S(1)} %broadcast_add_fusion.3, f32[128,128]{1,0:T(8,128)S(1)} %broadcast_subtract_fusion.3, s32[128,128]{1,0:T(8,128)S(1)} %bitcast.75), kind=kOutput, calls=%fused_computation.31 | convolution fusion | flops 92536832 | bytes 1048576 | tf_op jit(solution)/shard_map/rkp,rpb->rkb/dot_general | solution.py:26
  63.0 0.2 copy.52
  63.2 14.7 %fusion.22 = bf16[1024,1,256]{2,0,1:T(8,128)(2,1)S(1)} fusion(bf16[128,8,128]{2,1,0:T(8,128)(2,1)S(1)} %bitcast.59, f32[128,128]{1,0:T(8,128)S(1)} %bitcast.73, s32[128,128]{1,0:T(8,128)S(1)} %broadcast_add_fusion.2, f32[128,128]{1,0:T(8,128)S(1)} %broadcast_subtract_fusion.2, s32[128,128]{1,0:T(8,128)S(1)} %bitcast.71), kind=kOutput, calls=%fused_computation.32 | convolution fusion | flops 92536832 | bytes 1048576 | tf_op jit(solution)/shard_map/rkp,rpb->rkb/dot_general | solution.py:26
  78.0 0.2 copy.53
  78.2 14.7 %fusion.23 = bf16[1024,1,256]{2,0,1:T(8,128)(2,1)S(1)} fusion(bf16[128,8,128]{2,1,0:T(8,128)(2,1)S(1)} %bitcast.60, f32[128,128]{1,0:T(8,128)S(1)} %bitcast.69, s32[128,128]{1,0:T(8,128)S(1)} %broadcast_add_fusion.1, f32[128,128]{1,0:T(8,128)S(1)} %broadcast_subtract_fusion.1, s32[128,128]{1,0:T(8,128)S(1)} %bitcast.67), kind=kOutput, calls=%fused_computation.33 | convolution fusion | flops 92536832 | bytes 1048576 | tf_op jit(solution)/shard_map/rkp,rpb->rkb/dot_general | solution.py:26
  92.9 0.2 copy.54
  93.1 14.7 %fusion.24 = bf16[1024,1,256]{2,0,1:T(8,128)(2,1)S(1)} fusion(bf16[128,8,128]{2,1,0:T(8,128)(2,1)S(1)} %bitcast.61, f32[128,128]{1,0:T(8,128)S(1)} %bitcast.65, s32[128,128]{1,0:T(8,128)S(1)} %broadcast_add_fusion, f32[128,128]{1,0:T(8,128)S(1)} %broadcast_subtract_fusion, s32[128,128]{1,0:T(8,128)S(1)} %bitcast.63), kind=kOutput, calls=%fused_computation.34 | convolution fusion | flops 92536832 | bytes 1048576 | tf_op jit(solution)/shard_map/rkp,rpb->rkb/dot_general | solution.py:26
  107.8 0.2 copy.55
  108.0 10.9 %fusion.7 = f32[1024,4,256]{0,2,1:T(8,128)} fusion(bf16[128,8,4,1024]{3,2,1,0:T(4,128)(2,1)} %constant_dynamic-slice_fusion.5, bf16[1024,1,256]{0,2,1:T(8,128)(2,1)S(1)} %copy.55, bf16[1024,1,256]{0,2,1:T(8,128)(2,1)S(1)} %copy.54, bf16[1024,1,256]{0,2,1:T(8,128)(2,1)S(1)} %copy.53, bf16[1024,1,256]{0,2,1:T(8,128)(2,1)S(1)} %copy.52), kind=kOutput, calls=%fused_computation.19 | convolution fusion | flops 2150629376 | bytes 14680064 | tf_op jit(solution)/shard_map/cot,cob->tob/dot_general | solution.py:74
  118.9 5.2 %copy.57 = f32[1024,4,256]{2,1,0:T(4,128)} copy(f32[1024,4,256]{0,2,1:T(8,128)} %fusion.7) | data formatting | bytes 8388608 | tf_op jit(solution)/shard_map/cot,cob->tob/transpose | solution.py:74
  124.2 142.0 %all-reduce.3.cloned.1.call-done = f32[1024,4,256]{2,1,0:T(4,128)} async-done(((f32[1024,4,256]{2,1,0:T(4,128)}), f32[1024,4,256]{2,1,0:T(4,128)}) %all-reduce.3.cloned.1.call-update) | async-done | bytes 4194320
  266.2 1.6 constant_dynamic-slice_fusion.9
  (16 shorter events, 0.3 us)
Async XLA Ops:
  9.7 15.6 %all-to-all-start = ((s32[16,8,1]{1,2,0:T(1,128)}), s32[16,8,1]{1,2,0:T(1,128)S(1)}, u32[]{:S(2)}, u32[]{:S(2)}) async-start(s32[16,8,1]{1,2,0:T(1,128)} %bitcast.1), calls=%async_computation | async-start | bytes 16384 | tf_op jit(solution)/shard_map/all_to_all | solution.py:54
  25.3 12.0 %all-to-all-start.1 = ((bf16[16,8,1024]{2,1,0:T(8,128)(2,1)}), bf16[16,8,1024]{2,1,0:T(8,128)(2,1)S(1)}, u32[]{:S(2)}, u32[]{:S(2)}) async-start(bf16[16,8,1024]{2,1,0:T(8,128)(2,1)} %fusion.25), calls=%async_computation.1 | async-start | bytes 524288 | tf_op jit(solution)/shard_map/all_to_all | solution.py:53
  28.8 18.4 %reduce-scatter.2.cloned.1.call-start = ((), (), s32[]{:S(2)}) async-start(), calls=%async_computation.3 | async-start | bytes 1572864 | tf_op jit(solution)/shard_map/reduce_scatter | solution.py:63
  38.6 227.5 %all-reduce.3.cloned.1.call-start = ((), (), s32[]{:S(2)}) async-start(), calls=%async_computation.4 | async-start | bytes 8388608
Sparse Core Ops, SparseCore 0:
  38.8 6.4 reduce-scatter.1
  124.3 141.8 all-reduce.2
where the time goes:
time: 275 us
  waiting for transfers between devices  150 us (55%)
  matrix products  72.1 us (26%)
  local copies, waits for them, and re-layouts  20.6 us (7%)
  between operations  13.6 us (5%)
  starting transfers between devices  12 us (4%)
  other arithmetic  5.91 us (2%)
    unnamed x3, waiting for transfers between devices  142 us
    dot_general x4, matrix products, bin_rows(): jnp.einsum('rkp,rpb->rkb', row_rounded, weights, preferred_element_type=j...  58.9 us
    dot_general x1, matrix products, on_device(): jnp.einsum('cot,cob->tob', own_gains, arrived, preferred_element_type=jnp...  10.9 us
    dynamic_slice x1, local copies, waits for them, and re-layouts, on_device(): lax.dynamic_slice_in_dim(gain_table, first, share_rows, 0)  8.35 us
    all_to_all x1, starting transfers between devices, on_device(): lax.all_to_all(send_rows, 'gx', split_axis=0, concat_axis=0, tiled=True)  8.34 us
  transfers between devices with their start and end apart: 4, of which 3 were waited for; matrix products, arithmetic and copies ran while one was open for 6% of the time, Pallas kernels for 0%

commit v1 on v0

v1 whole, which is shorter than its diff:
```python
import functools

import jax
import jax.numpy as jnp
from jax import lax
from jax.experimental import pallas as pl
from jax.experimental.pallas import tpu as pltpu
from jax.sharding import PartitionSpec as P

NBIN = 256
LANES = 128
STEP = 512
F32 = jnp.float32
BF16 = jnp.bfloat16
VMEM = pl.BlockSpec(memory_space=pltpu.VMEM)


def iota(shape, axis):
    return lax.broadcasted_iota(jnp.int32, shape, axis)


def pack_kernel(slots, src_ref, own_ref, row_ref, cnt_ref, out_ref, held):
    strips, terms, panels = src_ref.shape
    shards = out_ref.shape[0]
    own_row = own_ref[...].astype(F32)
    same = iota((strips, strips), 0) == iota((strips, strips), 1)
    earlier = iota((strips, strips), 0) < iota((strips, strips), 1)
    own_col = jnp.sum(jnp.where(same, own_row, 0.0), axis=1, keepdims=True)
    cnt_col = jnp.sum(jnp.where(same, cnt_ref[...].astype(F32), 0.0), axis=1, keepdims=True)
    ranks = jnp.sum(
        jnp.where(jnp.logical_and(own_col == own_row, earlier), 1.0, 0.0), axis=0, keepdims=True
    )
    slot_row = own_row * slots + ranks
    total = shards * slots
    placed = iota((total, strips), 0).astype(F32) == slot_row
    placing = jnp.where(placed, 1.0, 0.0).astype(BF16)
    rows = (
        jnp.sum(jnp.where(placed, row_ref[...].astype(F32) + 1.0, 0.0), axis=1, keepdims=True) - 1.0
    )
    held[...] = src_ref[...].astype(F32).reshape(strips * terms, panels)
    live = iota((strips, panels), 1).astype(F32) < cnt_col
    for first in range(0, terms, 2):
        pair = []
        for term in (first, first + 1):
            masked = jnp.where(live, held[pl.ds(term, strips, stride=terms), :], 0.0).astype(BF16)
            moved = jnp.dot(placing, masked, preferred_element_type=F32)
            pair.append(moved.reshape(shards, slots, panels))
        out_ref[:, first * slots : (first + 2) * slots, :] = jnp.concatenate(pair, axis=1).astype(
            BF16
        )
    out_ref[:, terms * slots :, :] = (
        jnp.broadcast_to(rows, (total, panels)).reshape(shards, slots, panels).astype(BF16)
    )


PAIRS = 32


def gains_kernel(blocks, first_ref, view_ref, out_ref, held):
    count, pitch, lanes = held.shape
    group = view_ref.shape[0] // count
    held[:, :group, :] = view_ref[...].astype(F32).reshape(count, group, lanes)
    flat = held.reshape(count * pitch, lanes)
    for part in range(group // blocks):
        for turn in range(out_ref.shape[0]):
            taken = flat[pl.ds(first_ref[0] + turn + part * blocks, count, stride=pitch), :]
            out_ref[turn, :, part * lanes : (part + 1) * lanes] = taken.astype(BF16)


def signal_kernel(slots, terms, columns, *refs):
    got_refs, (bin_ref, frac_ref, gain_ref, out_ref) = refs[:columns], refs[columns : columns + 4]
    held, src, arr, gains, low, high, at, sem = refs[columns + 4 :]
    own, row_count, panels = bin_ref.shape
    devices, _, share, _ = out_ref.shape
    copies = [
        pltpu.make_async_copy(gain_ref.at[turn], gains.at[turn], sem.at[turn])
        for turn in range(own)
    ]
    for copy in copies:
        copy.start()
    low[...] = 1.0 - frac_ref[...]
    high[...] = frac_ref[...]
    at[...] = bin_ref[...].astype(F32)

    def taken(term):
        parts = [
            ref[:, term * slots : (term + 1) * slots, :].astype(F32).reshape(-1, panels)
            for ref in got_refs
        ]
        return jnp.concatenate(parts, axis=0)

    rows = taken(terms)
    hot_t = jnp.concatenate(
        [
            jnp.where(rows == (iota(rows.shape, 1) + start).astype(F32), 1.0, 0.0)
            for start in range(0, row_count, panels)
        ],
        axis=1,
    )
    hot = hot_t.T.astype(BF16)
    for term in range(terms):
        held[pl.ds(term, row_count, stride=terms), :] = jnp.dot(
            hot, taken(term).astype(BF16), preferred_element_type=F32
        )
    src[...] = held[...].astype(BF16)

    half = 2 * terms
    upper = iota((half, panels), 0) < terms
    place = iota((half, panels), 0).astype(F32)

    def spread(value):
        return jnp.broadcast_to(value, (half, panels))

    def weights(turn, row):
        here = at[turn, pl.ds(row, 1), :]
        tile = jnp.floor(here * (1.0 / half))
        inner = spread(here - half * tile)
        tile = spread(tile).astype(BF16)
        low_w, high_w = spread(low[turn, pl.ds(row, 1), :]), spread(high[turn, pl.ds(row, 1), :])
        body = jnp.where(
            place == inner, low_w, jnp.where(place == inner + 1.0, high_w, 0.0)
        ).astype(BF16)
        spill = jnp.where(place + float(half - 1) == inner, high_w, 0.0).astype(BF16)
        zero = jnp.zeros((half, panels), BF16)
        tiles, before = [], None
        for index in range(NBIN // half):
            match = tile == jnp.full((half, panels), index, BF16)
            rest = zero if before is None else jnp.where(before, spill, zero)
            tiles.append(jnp.where(match, body, rest))
            before = match
        return jnp.concatenate(tiles, axis=0)

    for turn in range(own):

        def step(index, carry, turn=turn):
            for inner in range(PAIRS):
                pair = index * PAIRS + inner
                where = pl.ds(pl.multiple_of(pair * half, half), half)
                rows16 = src[where, :]
                zero = jnp.zeros_like(rows16)
                lhs = jnp.concatenate(
                    [jnp.where(upper, rows16, zero), jnp.where(upper, zero, rows16)], axis=1
                )
                rhs = jnp.concatenate(
                    [weights(turn, 2 * pair), weights(turn, 2 * pair + 1)], axis=1
                )
                binned = lax.dot_general(
                    lhs, rhs, (((1,), (1,)), ((), ())), preferred_element_type=F32
                )
                arr[where, :] = binned.astype(BF16)
            return carry

        lax.fori_loop(0, row_count // (2 * PAIRS), step, 0)
        copies[turn].wait()
        out_t = lax.dot_general(
            arr[...], gains[turn], (((0,), (0,)), ((), ())), preferred_element_type=F32
        )
        out_ref[:, turn] = out_t.T.astype(BF16).reshape(devices, share, NBIN)


def on_device(sources, owners, strip_rows, panel_counts, arrival_bins, arrival_fracs, gain_table):
    strips, terms, panels = sources.shape
    shards = lax.axis_size("gx")
    columns = lax.axis_size("gy")
    cap = 2 * strips // shards
    slots = -(-cap // 8) * 8
    rows_here, blocks = arrival_bins.shape[:2]
    observers = gain_table.shape[3]
    own = blocks // columns
    devices = shards * columns
    assert rows_here <= 256 and blocks % columns == 0

    send = pl.pallas_call(
        functools.partial(pack_kernel, slots),
        out_shape=jax.ShapeDtypeStruct((shards, (terms + 1) * slots, panels), BF16),
        in_specs=[VMEM] * 4,
        out_specs=VMEM,
        scratch_shapes=[pltpu.VMEM((strips * terms, panels), F32)],
        name="pack",
    )(sources, owners.reshape(1, strips), strip_rows.reshape(1, strips), panel_counts.reshape(1, strips))

    got = lax.all_to_all(send, "gx", split_axis=0, concat_axis=0, tiled=True)
    first = lax.axis_index("gy") * own
    group = blocks * (observers // LANES)
    view = (
        gain_table.reshape(rows_here * terms, blocks, observers // LANES, LANES)
        .transpose(0, 2, 1, 3)
        .reshape(rows_here * terms * group, LANES)
    )
    own_gains = pl.pallas_call(
        functools.partial(gains_kernel, blocks),
        out_shape=jax.ShapeDtypeStruct((own, rows_here * terms, observers), BF16),
        grid_spec=pltpu.PrefetchScalarGridSpec(
            num_scalar_prefetch=1,
            grid=(rows_here * terms // STEP,),
            in_specs=[pl.BlockSpec((STEP * group, LANES), lambda i, f: (i, 0))],
            out_specs=pl.BlockSpec((own, STEP, observers), lambda i, f: (0, i, 0)),
            scratch_shapes=[pltpu.VMEM((STEP, group + 8, LANES), F32)],
        ),
        name="gains",
        cost_estimate=pl.CostEstimate(
            flops=20 * gain_table.size, bytes_accessed=3 * gain_table.size, transcendentals=0
        ),
    )(first.reshape(1), view)
    bins = jnp.transpose(lax.dynamic_slice_in_dim(arrival_bins, first, own, 1), (1, 0, 2))
    fracs = jnp.transpose(lax.dynamic_slice_in_dim(arrival_fracs, first, own, 1), (1, 0, 2))
    got, own_gains, bins, fracs = lax.optimization_barrier((got, own_gains, bins, fracs))
    parts = [got]
    for turn in range(1, columns):
        parts.append(
            lax.ppermute(got, "gy", [(i, (i + turn) % columns) for i in range(columns)])
        )
    share = observers // devices
    partial = pl.pallas_call(
        functools.partial(signal_kernel, slots, terms, columns),
        out_shape=jax.ShapeDtypeStruct((devices, own, share, NBIN), BF16),
        in_specs=[VMEM] * (columns + 2) + [pl.BlockSpec(memory_space=pltpu.HBM)],
        out_specs=VMEM,
        scratch_shapes=[
            pltpu.VMEM((rows_here * terms, panels), F32),
            pltpu.VMEM((rows_here * terms, panels), BF16),
            pltpu.VMEM((rows_here * terms, NBIN), BF16),
            pltpu.VMEM((own, rows_here * terms, observers), BF16),
            pltpu.VMEM((own, rows_here, panels), F32),
            pltpu.VMEM((own, rows_here, panels), F32),
            pltpu.VMEM((own, rows_here, panels), F32),
            pltpu.SemaphoreType.DMA((own,)),
        ],
        name="signal",
        compiler_params=pltpu.CompilerParams(vmem_limit_bytes=48 << 20),
        cost_estimate=pl.CostEstimate(
            flops=2 * own * rows_here * terms * NBIN * (observers + panels * 8),
            bytes_accessed=2 * own * rows_here * terms * observers,
            transcendentals=0,
        ),
    )(*parts, bins, fracs, own_gains)
    got = lax.all_to_all(partial, ("gx", "gy"), split_axis=0, concat_axis=0, tiled=True)
    sums = jnp.sum(got.reshape(shards, columns, own, share, NBIN).astype(F32), axis=0)
    return jnp.transpose(sums.reshape(blocks, share, NBIN), (1, 0, 2))


def solution(mesh):
    placed = (
        P(("gx", "gy"), None, None),
        P(("gx", "gy"), None),
        P(("gx", "gy")),
        P(("gx", "gy")),
        P("gx", None, None),
        P("gx", None, None),
        P("gx", None, None, None),
    )
    return jax.shard_map(
        on_device,
        mesh=mesh,
        in_specs=placed,
        out_specs=P(("gx", "gy"), None, None),
        check_vma=False,
    )
```

time: 275 us -> 71.3 us (0.26)
  waiting for transfers between devices: 150 us -> 1.58 us
  matrix products: 72.1 us -> 0 us
  blocking collectives: 0 us -> 31.9 us
  Pallas kernels: 0 us -> 26.9 us
  local copies, waits for them, and re-layouts: 20.6 us -> 2.06 us
  between operations: 13.6 us -> 0.07 us
  other arithmetic: 5.91 us -> 0.19 us
  starting transfers between devices: 12 us -> 8.35 us
    unnamed x3 -> x0, waiting for transfers between devices: 142 us -> none
    dot_general x7 -> x0, matrix products: 72.1 us -> none  [the longest x4 58.9 us: bin_rows(): jnp.einsum('rkp,rpb->rkb', row_rounded, weights, preferred_element_type=j...]
    all_to_all x0 -> x1, blocking collectives: none -> 31.9 us  [on_device(): lax.all_to_all(partial, ('gx', 'gy'), split_axis=0, concat_axis=0, tiled=...]
    pallas_call x0 -> x3, Pallas kernels: none -> 26.9 us  [the longest x1 13.1 us: on_device(): pl.pallas_call(functools.partial(signal_kernel, slots, terms, columns), o...]
    all_to_all x2 -> x1, waiting for transfers between devices: 8.41 us -> 0.01 us  [on_device(): got = lax.all_to_all(send, 'gx', split_axis=0, concat_axis=0, tiled=True)]
    dynamic_slice x1 -> x2, local copies, waits for them, and re-layouts: 8.35 us -> 1.28 us  [the longest x1 1.16 us: on_device(): lax.dynamic_slice_in_dim(arrival_fracs, first, own, 1)]
    transpose x1 -> x0, local copies, waits for them, and re-layouts: 5.24 us -> none  [on_device(): jnp.einsum('cot,cob->tob', own_gains, arrived, preferred_element_type=jnp...]
    all_to_all x2 -> x1, starting transfers between devices: 11.9 us -> 8.34 us  [on_device(): got = lax.all_to_all(send, 'gx', split_axis=0, concat_axis=0, tiled=True)]
  transfers between devices with their start and end apart: 4 -> 2, of which waited for: 3 -> 1; matrix products, arithmetic and copies ran while one was open for 6% -> 2% of each run, Pallas kernels for 0% -> 17%
where the time goes in v1:
time: 71.3 us; the launch traced here: 71 us
  blocking collectives  31.9 us (45%)
  Pallas kernels  26.9 us (38%)
  starting transfers between devices  8.35 us (12%)
  local copies, waits for them, and re-layouts  2.06 us (3%)
  waiting for transfers between devices  1.58 us (2%)
    all_to_all x1, blocking collectives, on_device(): lax.all_to_all(partial, ('gx', 'gy'), split_axis=0, concat_axis=0, tiled=...  31.9 us
    pallas_call x1, Pallas kernels, on_device(): pl.pallas_call(functools.partial(signal_kernel, slots, terms, columns), o...  13.1 us
    pallas_call x1, Pallas kernels, on_device(): pl.pallas_call(functools.partial(gains_kernel, blocks), out_shape=jax.Sha...  11.8 us
    all_to_all x1, starting transfers between devices, on_device(): got = lax.all_to_all(send, 'gx', split_axis=0, concat_axis=0, tiled=True)  8.34 us
    pallas_call x1, Pallas kernels, on_device(): pl.pallas_call(functools.partial(pack_kernel, slots), out_shape=jax.Shape...  2.03 us
    ppermute x1, waiting for transfers between devices, on_device(): lax.ppermute(got, 'gy', [(i, (i + turn) % columns) for i in range(columns)])  1.58 us
  transfers between devices with their start and end apart: 2, of which 1 were waited for; matrix products, arithmetic and copies ran while one was open for 2% of the time, Pallas kernels for 17%

profile of v1, /device:TPU:0, one launch (start us, length us, event | category | flops | bytes accessed | tf_op | source)
XLA Modules:
  0.0 71.0 jit_solution(14094215988027167566)
XLA Ops:
  0.0 0.0 copy-start
  0.0 2.0 %pack.1 = bf16[16,72,128]{2,1,0:T(8,128)(2,1)} custom-call(bf16[64,8,128]{2,1,0:T(8,128)(2,1)} %src_ref.1, s32[1,64]{1,0:T(1,128)} %bitcast.26, s32[1,64]{1,0:T(1,128)} %bitcast.27, s32[1,64]{1,0:T(1,128)} %bitcast.28), custom_call_target="tpu_custom_call" | custom-call | tf_op jit(solution)/shard_map/pack/pallas_call | solution.py:173
  2.0 8.3 %all-to-all-start = ((bf16[16,72,128]{2,1,0:T(8,128)(2,1)}), bf16[16,72,128]{2,1,0:T(8,128)(2,1)S(1)}, u32[]{:S(2)}, u32[]{:S(2)}) async-start(bf16[16,72,128]{2,1,0:T(8,128)(2,1)} %pack.1), calls=%async_computation | async-start | bytes 589824 | tf_op jit(solution)/shard_map/all_to_all | solution.py:182
  10.4 0.0 copy-done
  10.4 0.1 constant_dynamic-slice_fusion.1
  10.5 1.2 %constant_dynamic-slice_fusion = f32[256,2,128]{2,1,0:T(2,128)S(1)} fusion(f32[256,4,128]{2,1,0:T(4,128)} %param.12, s32[]{:T(128)S(6)} %select_n.4), kind=kLoop, calls=%fused_computation.4 | loop fusion | bytes 524292 | tf_op jit(solution)/shard_map/dynamic_slice | solution.py:206
  11.7 11.8 %gains.1.refs_4_ = bf16[2,2048,1024]{2,1,0:T(8,128)(2,1)} custom-call(s32[1]{0:T(128)} %bitcast.3.first_ref, bf16[65536,128]{1,0:T(8,128)(2,1)} %bitcast.23), custom_call_target="tpu_custom_call" | custom-call | flops 167772160 | bytes 25165824 | tf_op jit(solution)/shard_map/gains/pallas_call | solution.py:190
  23.5 0.0 all-to-all-done.refs_0_
  23.5 0.0 collective-permute-start
  23.5 1.6 %collective-permute-done.refs_1_ = bf16[16,72,128]{2,1,0:T(8,128)(2,1)S(1)} collective-permute-done((bf16[16,72,128]{2,1,0:T(8,128)(2,1)S(1)}, bf16[16,72,128]{2,1,0:T(8,128)(2,1)S(1)}, u32[]{:S(2)}, u32[]{:S(2)}) %collective-permute-start) | collective-permute-done | bytes 294944 | tf_op jit(solution)/shard_map/ppermute | solution.py:211
  25.1 13.1 %signal.1 = bf16[32,2,32,256]{3,2,1,0:T(8,128)(2,1)S(1)} custom-call(bf16[16,72,128]{2,1,0:T(8,128)(2,1)S(1)} %all-to-all-done.refs_0_, bf16[16,72,128]{2,1,0:T(8,128)(2,1)S(1)} %collective-permute-done.refs_1_, s32[2,256,128]{2,1,0:T(8,128)S(1)} %bitcast.21, f32[2,256,128]{2,1,0:T(8,128)S(1)} %bitcast.22, bf16[2,2048,1024]{2,1,0:T(8,128)(2,1)} %gains.1.refs_4_), custom_call_target="tpu_custom_call" | custom-call | flops 4294967296 | bytes 8388608 | tf_op jit(solution)/shard_map/signal/pallas_call | solution.py:214
  38.2 31.9 %all_to_all.10 = bf16[32,2,32,256]{3,2,1,0:T(8,128)(2,1)S(1)} all-to-all(bf16[32,2,32,256]{3,2,1,0:T(8,128)(2,1)S(1)} %signal.1), channel_id=1, replica_groups=mesh['gx'=16,'gy'=2] {'gx','gy'}, dimensions={0} | all-to-all | bytes 2097152 | tf_op jit(solution)/shard_map/all_to_all | solution.py:237
  70.1 0.2 convert_reduce_fusion
  70.3 0.7 %copy.22 = f32[4,32,256]{2,0,1:T(4,128)} copy(f32[4,32,256]{2,1,0:T(8,128)S(1)} %bitcast.25) | data formatting | bytes 262144 | tf_op jit(solution)/shard_map/reshape | solution.py:239
  (2 shorter events, 0.0 us)
Async XLA Ops:
  0.0 10.4 %copy-start = (s32[256,4,128]{2,1,0:T(4,128)S(1)}, s32[256,4,128]{2,1,0:T(4,128)}, u32[]{:S(2)}) copy-start(s32[256,4,128]{2,1,0:T(4,128)} %param.11) | copy-start | bytes 1572868
  2.0 21.5 %all-to-all-start = ((bf16[16,72,128]{2,1,0:T(8,128)(2,1)}), bf16[16,72,128]{2,1,0:T(8,128)(2,1)S(1)}, u32[]{:S(2)}, u32[]{:S(2)}) async-start(bf16[16,72,128]{2,1,0:T(8,128)(2,1)} %pack.1), calls=%async_computation | async-start | bytes 589824 | tf_op jit(solution)/shard_map/all_to_all | solution.py:182
  23.5 1.6 %collective-permute-start = (bf16[16,72,128]{2,1,0:T(8,128)(2,1)S(1)}, bf16[16,72,128]{2,1,0:T(8,128)(2,1)S(1)}, u32[]{:S(2)}, u32[]{:S(2)}) collective-permute-start(bf16[16,72,128]{2,1,0:T(8,128)(2,1)S(1)} %all-to-all-done.refs_0_), channel_id=1, source_target_pairs={{0,1},{1,0},{2,3},{3,2},{4,5},{5,4},{6,7},{7,6},{8,9},{9,8},{10,11... | collective-permute-start | bytes 884744 | tf_op jit(solution)/shard_map/ppermute | solution.py:211

commit v2 on v1

v2 whole, which is shorter than its diff:
```python
import functools

import jax
import jax.numpy as jnp
from jax import lax
from jax.experimental import pallas as pl
from jax.experimental.pallas import tpu as pltpu
from jax.sharding import PartitionSpec as P

NBIN = 256
LANES = 128
STEP = 128
DEPTH = 8
SPARE = 4
F32 = jnp.float32
BF16 = jnp.bfloat16
VMEM = pl.BlockSpec(memory_space=pltpu.VMEM)
SMEM = pl.BlockSpec(memory_space=pltpu.SMEM)
HBM = pl.BlockSpec(memory_space=pltpu.HBM)


def iota(shape, axis):
    return lax.broadcasted_iota(jnp.int32, shape, axis)


def pack_kernel(slots, src_ref, own_ref, row_ref, cnt_ref, out_ref, held):
    strips, terms, panels = src_ref.shape
    shards = out_ref.shape[0]
    own_row = own_ref[...].astype(F32)
    same = iota((strips, strips), 0) == iota((strips, strips), 1)
    earlier = iota((strips, strips), 0) < iota((strips, strips), 1)
    own_col = jnp.sum(jnp.where(same, own_row, 0.0), axis=1, keepdims=True)
    cnt_col = jnp.sum(jnp.where(same, cnt_ref[...].astype(F32), 0.0), axis=1, keepdims=True)
    ranks = jnp.sum(
        jnp.where(jnp.logical_and(own_col == own_row, earlier), 1.0, 0.0), axis=0, keepdims=True
    )
    slot_row = own_row * slots + ranks
    total = shards * slots
    placed = iota((total, strips), 0).astype(F32) == slot_row
    placing = jnp.where(placed, 1.0, 0.0).astype(BF16)
    rows = (
        jnp.sum(jnp.where(placed, row_ref[...].astype(F32) + 1.0, 0.0), axis=1, keepdims=True) - 1.0
    )
    held[...] = src_ref[...].astype(F32).reshape(strips * terms, panels)
    live = iota((strips, panels), 1).astype(F32) < cnt_col
    for first in range(0, terms, 2):
        pair = []
        for term in (first, first + 1):
            masked = jnp.where(live, held[pl.ds(term, strips, stride=terms), :], 0.0).astype(BF16)
            moved = jnp.dot(placing, masked, preferred_element_type=F32)
            pair.append(moved.reshape(shards, slots, panels))
        out_ref[:, first * slots : (first + 2) * slots, :] = jnp.concatenate(pair, axis=1).astype(
            BF16
        )
    out_ref[:, terms * slots :, :] = (
        jnp.broadcast_to(rows, (total, panels)).reshape(shards, slots, panels).astype(BF16)
    )


PAIRS = 64


def gains_kernel(blocks, first_ref, view_ref, out_ref, inward, outward, in_sem, out_sem):
    depth, taken_rows, lanes = inward.shape
    spare, own, count, observers = outward.shape
    tiles = observers // lanes
    group = taken_rows // count
    steps = view_ref.shape[0] // taken_rows
    chunk = 8 * group
    shape = (own * tiles * 8, chunk)
    to, come = iota(shape, 0), iota(shape, 1)
    block = first_ref[0] + to // (8 * tiles)
    wanted = (to % 8) * group + (to // 8 % tiles) * blocks + block
    pick = jnp.where(come == wanted, 1.0, 0.0).astype(BF16)

    def fetch(step):
        slot = lax.rem(step, depth)
        return pltpu.make_async_copy(
            view_ref.at[pl.ds(pl.multiple_of(step * taken_rows, taken_rows), taken_rows), :],
            inward.at[slot],
            in_sem.at[slot],
        )

    def leave(step):
        slot = lax.rem(step, spare)
        return pltpu.make_async_copy(
            outward.at[slot],
            out_ref.at[:, pl.ds(pl.multiple_of(step * count, count), count), :],
            out_sem.at[slot],
        )

    for step in range(depth - 1):
        fetch(step).start()

    def body(step, carry):
        @pl.when(step + depth - 1 < steps)
        def _():
            fetch(step + depth - 1).start()

        fetch(step).wait()

        @pl.when(step >= spare)
        def _():
            leave(step - spare).wait()

        slot, held = lax.rem(step, spare), lax.rem(step, depth)
        for at in range(0, count, 16):
            pair = jnp.concatenate(
                [
                    inward[held, at * group : at * group + chunk, :],
                    inward[held, at * group + chunk : at * group + 2 * chunk, :],
                ],
                axis=1,
            )
            taken = jnp.dot(pick, pair, preferred_element_type=F32)
            for turn in range(own):
                for tile in range(tiles):
                    start = (turn * tiles + tile) * 8
                    both = jnp.concatenate(
                        [taken[start : start + 8, :lanes], taken[start : start + 8, lanes:]], axis=0
                    )
                    outward[slot, turn, at : at + 16, tile * lanes : (tile + 1) * lanes] = (
                        both.astype(BF16)
                    )
        leave(step).start()
        return carry

    lax.fori_loop(0, steps, body, 0)
    for step in range(steps - spare, steps):
        leave(step).wait()


def sum_rows(slots, terms, got_refs, held, src):
    panels = src.shape[1]
    row_count = src.shape[0] // terms

    def taken(term):
        parts = [
            ref[:, term * slots : (term + 1) * slots, :].astype(F32).reshape(-1, panels)
            for ref in got_refs
        ]
        return jnp.concatenate(parts, axis=0)

    rows = taken(terms)
    hot_t = jnp.concatenate(
        [
            jnp.where(rows == (iota(rows.shape, 1) + start).astype(F32), 1.0, 0.0)
            for start in range(0, row_count, panels)
        ],
        axis=1,
    )
    hot = hot_t.T.astype(BF16)
    for term in range(terms):
        held[pl.ds(term, row_count, stride=terms), :] = jnp.dot(
            hot, taken(term).astype(BF16), preferred_element_type=F32
        )
    src[...] = held[...].astype(BF16)


def signal_kernel(slots, terms, columns, lines, turn, *refs):
    opening = turn == 0
    if opening:
        got_refs, refs = refs[:columns], refs[columns:]
        block_ref, bin_ref, frac_ref, gain_ref, out_ref, src, held, arr, gains, turned, sem = refs
    else:
        block_ref, src, bin_ref, frac_ref, gain_ref, out_ref, arr, gains, turned, sem = refs
    row_count, _, panels = bin_ref.shape
    targets = out_ref.shape[0]
    copy = pltpu.make_async_copy(gain_ref.at[turn], gains, sem)
    copy.start()
    if opening:
        sum_rows(slots, terms, got_refs, held, src)
    block = block_ref[0] + turn
    half = 2 * terms
    upper = iota((half, panels), 0) < terms
    place = iota((half, panels), 0).astype(F32)

    def spread(value):
        return jnp.broadcast_to(value, (half, panels))

    def weights(row):
        here = bin_ref[row, pl.ds(block, 1), :].astype(F32)
        past = frac_ref[row, pl.ds(block, 1), :]
        tile = jnp.floor(here * (1.0 / half))
        inner = spread(here - half * tile)
        tile = spread(tile).astype(BF16)
        low_w, high_w = spread(1.0 - past), spread(past)
        body = jnp.where(
            place == inner, low_w, jnp.where(place == inner + 1.0, high_w, 0.0)
        ).astype(BF16)
        spill = jnp.where(place + float(half - 1) == inner, high_w, 0.0).astype(BF16)
        zero = jnp.zeros((half, panels), BF16)
        tiles, before = [], None
        for index in range(NBIN // half):
            match = tile == jnp.full((half, panels), index, BF16)
            rest = zero if before is None else jnp.where(before, spill, zero)
            tiles.append(jnp.where(match, body, rest))
            before = match
        return jnp.concatenate(tiles, axis=0)

    def step(index, carry):
        for inner in range(PAIRS):
            pair = index * PAIRS + inner
            where = pl.ds(pl.multiple_of(pair * half, half), half)
            rows16 = src[where, :]
            zero = jnp.zeros_like(rows16)
            lhs = jnp.concatenate(
                [jnp.where(upper, rows16, zero), jnp.where(upper, zero, rows16)], axis=1
            )
            rhs = jnp.concatenate([weights(2 * pair), weights(2 * pair + 1)], axis=1)
            if inner % 3 < 2:
                turned[inner] = rhs.T
                binned = jnp.dot(lhs, turned[inner], preferred_element_type=F32)
            else:
                binned = lax.dot_general(
                    lhs, rhs, (((1,), (1,)), ((), ())), preferred_element_type=F32
                )
            arr[where, :] = binned.astype(BF16)
        return carry

    lax.fori_loop(0, row_count // (2 * PAIRS), step, 0)
    copy.wait()
    out_t = lax.dot_general(
        arr[...], gains[...], (((0,), (0,)), ((), ())), preferred_element_type=F32
    )
    out = out_t.T.astype(BF16)
    piece = out.shape[0] // (targets * lines)
    for line in range(lines):
        for target in range(targets):
            start = (line * targets + target) * piece
            out_ref[target, line * piece : (line + 1) * piece, :] = out[start : start + piece, :]


def on_device(sources, owners, strip_rows, panel_counts, arrival_bins, arrival_fracs, gain_table):
    strips, terms, panels = sources.shape
    shards = lax.axis_size("gx")
    columns = lax.axis_size("gy")
    cap = 2 * strips // shards
    slots = -(-cap // 8) * 8
    rows_here, blocks = arrival_bins.shape[:2]
    observers = gain_table.shape[3]
    own = blocks // columns
    devices = shards * columns
    assert rows_here <= 256 and blocks % columns == 0

    send = pl.pallas_call(
        functools.partial(pack_kernel, slots),
        out_shape=jax.ShapeDtypeStruct((shards, (terms + 1) * slots, panels), BF16),
        in_specs=[VMEM] * 4,
        out_specs=VMEM,
        scratch_shapes=[pltpu.VMEM((strips * terms, panels), F32)],
        name="pack",
    )(sources, owners.reshape(1, strips), strip_rows.reshape(1, strips), panel_counts.reshape(1, strips))

    got = lax.all_to_all(send, "gx", split_axis=0, concat_axis=0, tiled=True)
    first = lax.axis_index("gy") * own
    group = blocks * (observers // LANES)
    view = (
        gain_table.reshape(rows_here * terms, blocks, observers // LANES, LANES)
        .transpose(0, 2, 1, 3)
        .reshape(rows_here * terms * group, LANES)
    )
    own_gains = pl.pallas_call(
        functools.partial(gains_kernel, blocks),
        out_shape=jax.ShapeDtypeStruct((own, rows_here * terms, observers), BF16),
        in_specs=[SMEM, HBM],
        out_specs=HBM,
        scratch_shapes=[
            pltpu.VMEM((DEPTH, STEP * group, LANES), BF16),
            pltpu.VMEM((SPARE, own, STEP, observers), BF16),
            pltpu.SemaphoreType.DMA((DEPTH,)),
            pltpu.SemaphoreType.DMA((SPARE,)),
        ],
        name="gains",
        cost_estimate=pl.CostEstimate(
            flops=20 * gain_table.size, bytes_accessed=3 * gain_table.size, transcendentals=0
        ),
    )(first.reshape(1), view)
    got, own_gains = lax.optimization_barrier((got, own_gains))
    parts = [got]
    for turn in range(1, columns):
        parts.append(
            lax.ppermute(got, "gy", [(i, (i + turn) % columns) for i in range(columns)])
        )
    share = observers // devices
    planes = 1
    while planes * planes < shards:
        planes *= 2
    lines = shards // planes
    in_plane = [[line * planes + i for i in range(planes)] for line in range(lines)]
    in_line = [
        [(line * planes + i) * columns + j for line in range(lines) for j in range(columns)]
        for i in range(planes)
    ]
    plane_sums, row_sources = [], None
    for turn in range(own):
        opening = turn == 0
        partial = jax.ShapeDtypeStruct((planes, lines * columns * share, NBIN), BF16)
        source = jax.ShapeDtypeStruct((rows_here * terms, panels), BF16)
        made = pl.pallas_call(
            functools.partial(signal_kernel, slots, terms, columns, lines, turn),
            out_shape=(partial, source) if opening else (partial,),
            in_specs=([VMEM] * columns + [SMEM] if opening else [SMEM, VMEM]) + [VMEM] * 2 + [HBM],
            out_specs=(VMEM, VMEM) if opening else (VMEM,),
            scratch_shapes=([pltpu.VMEM((rows_here * terms, panels), F32)] if opening else [])
            + [
                pltpu.VMEM((rows_here * terms, NBIN), BF16),
                pltpu.VMEM((rows_here * terms, observers), BF16),
                pltpu.VMEM((PAIRS, 2 * panels, NBIN), BF16),
                pltpu.SemaphoreType.DMA,
            ],
            name="signal",
            compiler_params=pltpu.CompilerParams(vmem_limit_bytes=48 << 20),
            cost_estimate=pl.CostEstimate(
                flops=2 * rows_here * terms * NBIN * (observers + panels * 8),
                bytes_accessed=2 * rows_here * terms * observers,
                transcendentals=0,
            ),
        )(
            *(parts + [first.reshape(1)] if opening else [first.reshape(1), row_sources]),
            arrival_bins,
            arrival_fracs,
            own_gains,
        )
        if opening:
            row_sources = made[1]
        met = lax.all_to_all(
            made[0], "gx", split_axis=0, concat_axis=0, axis_index_groups=in_plane, tiled=True
        )
        plane_sums.append(
            jnp.sum(met.astype(F32), axis=0).astype(BF16).reshape(lines * columns, share, NBIN)
        )
    met = lax.all_to_all(
        jnp.stack(plane_sums, axis=1),
        ("gx", "gy"),
        split_axis=0,
        concat_axis=0,
        axis_index_groups=in_line,
        tiled=True,
    )
    sums = jnp.sum(met.reshape(lines, columns, own, share, NBIN).astype(F32), axis=0)
    return jnp.transpose(sums.reshape(blocks, share, NBIN), (1, 0, 2))


def solution(mesh):
    placed = (
        P(("gx", "gy"), None, None),
        P(("gx", "gy"), None),
        P(("gx", "gy")),
        P(("gx", "gy")),
        P("gx", None, None),
        P("gx", None, None),
        P("gx", None, None, None),
    )
    return jax.shard_map(
        on_device,
        mesh=mesh,
        in_specs=placed,
        out_specs=P(("gx", "gy"), None, None),
        check_vma=False,
    )
```

time: 71.3 us -> 66.6 us (0.934)
  blocking collectives: 31.9 us -> 13.3 us
  waiting for transfers between devices: 1.58 us -> 13.4 us
  starting transfers between devices: 8.35 us -> 15.3 us
  Pallas kernels: 26.9 us -> 23.2 us
  local copies, waits for them, and re-layouts: 2.06 us -> 0.75 us
    all_to_all x1, blocking collectives: 31.9 us -> 13.3 us  [on_device(): lax.all_to_all(jnp.stack(plane_sums, axis=1), ('gx', 'gy'), split_axis=0,...]
    all_to_all x0 -> x2, waiting for transfers between devices: none -> 10.7 us  [on_device(): lax.all_to_all(made[0], 'gx', split_axis=0, concat_axis=0, axis_index_gro...]
    all_to_all x0 -> x2, starting transfers between devices: none -> 6.95 us  [on_device(): lax.all_to_all(made[0], 'gx', split_axis=0, concat_axis=0, axis_index_gro...]
    pallas_call x1, Pallas kernels: 11.8 us -> 9.56 us  [on_device(): pl.pallas_call(functools.partial(gains_kernel, blocks), out_shape=jax.Sha...]
    pallas_call x1 -> x2, Pallas kernels: 13.1 us -> 11.6 us  [on_device(): pl.pallas_call(functools.partial(signal_kernel, slots, terms, columns, li...]
    dynamic_slice x2 -> x0, local copies, waits for them, and re-layouts: 1.28 us -> none  [the longest x1 1.16 us: on_device(): lax.dynamic_slice_in_dim(arrival_fracs, first, own, 1)]
    all_to_all x1, waiting for transfers between devices: 0.01 us -> 1.11 us  [on_device(): got = lax.all_to_all(send, 'gx', split_axis=0, concat_axis=0, tiled=True)]
  transfers between devices with their start and end apart: 2 -> 4, of which waited for: 1 -> 4; matrix products, arithmetic and copies ran while one was open for 2% -> 0% of each run, Pallas kernels for 17% -> 23%
where the time goes in v2:
time: 66.6 us; the launch traced here: 66.2 us
  Pallas kernels  23.2 us (35%)
  starting transfers between devices  15.3 us (23%)
  waiting for transfers between devices  13.4 us (20%)
  blocking collectives  13.3 us (20%)
  local copies, waits for them, and re-layouts  0.75 us (1%)
    all_to_all x1, blocking collectives, on_device(): lax.all_to_all(jnp.stack(plane_sums, axis=1), ('gx', 'gy'), split_axis=0,...  13.3 us
    pallas_call x2, Pallas kernels, on_device(): pl.pallas_call(functools.partial(signal_kernel, slots, terms, columns, li...  11.6 us
    all_to_all x2, waiting for transfers between devices, on_device(): lax.all_to_all(made[0], 'gx', split_axis=0, concat_axis=0, axis_index_gro...  10.7 us
    pallas_call x1, Pallas kernels, on_device(): pl.pallas_call(functools.partial(gains_kernel, blocks), out_shape=jax.Sha...  9.56 us
    all_to_all x1, starting transfers between devices, on_device(): got = lax.all_to_all(send, 'gx', split_axis=0, concat_axis=0, tiled=True)  8.34 us
    all_to_all x2, starting transfers between devices, on_device(): lax.all_to_all(made[0], 'gx', split_axis=0, concat_axis=0, axis_index_gro...  6.95 us
    pallas_call x1, Pallas kernels, on_device(): pl.pallas_call(functools.partial(pack_kernel, slots), out_shape=jax.Shape...  2.05 us
    ppermute x1, waiting for transfers between devices, on_device(): lax.ppermute(got, 'gy', [(i, (i + turn) % columns) for i in range(columns)])  1.58 us
  transfers between devices with their start and end apart: 4, of which 4 were waited for; matrix products, arithmetic and copies ran while one was open for 0% of the time, Pallas kernels for 23%

profile of v2, /device:TPU:0, one launch (start us, length us, event | category | flops | bytes accessed | tf_op | source)
XLA Modules:
  0.0 66.2 jit_solution(14227029627163226184)
XLA Ops:
  0.0 0.0 copy-start.1
  0.0 0.0 copy-start
  0.0 2.1 %pack.1 = bf16[16,72,128]{2,1,0:T(8,128)(2,1)} custom-call(bf16[64,8,128]{2,1,0:T(8,128)(2,1)} %src_ref.1, s32[1,64]{1,0:T(1,128)} %bitcast.22, s32[1,64]{1,0:T(1,128)} %bitcast.23, s32[1,64]{1,0:T(1,128)} %bitcast.24), custom_call_target="tpu_custom_call" | custom-call | tf_op jit(solution)/shard_map/pack/pallas_call | solution.py:246
  2.1 8.3 %all-to-all-start = ((bf16[16,72,128]{2,1,0:T(8,128)(2,1)}), bf16[16,72,128]{2,1,0:T(8,128)(2,1)S(1)}, u32[]{:S(2)}, u32[]{:S(2)}) async-start(bf16[16,72,128]{2,1,0:T(8,128)(2,1)} %pack.1), calls=%async_computation | async-start | bytes 589824 | tf_op jit(solution)/shard_map/all_to_all | solution.py:255
  10.4 9.6 %gains.1.refs_5_.refs_4_ = bf16[2,2048,1024]{2,1,0:T(8,128)(2,1)} custom-call(s32[1]{0:T(128)} %bitcast.3.first_ref.refs_2_.refs_0_, bf16[65536,128]{1,0:T(8,128)(2,1)} %bitcast.17), custom_call_target="tpu_custom_call" | custom-call | flops 167772160 | bytes 25165824 | tf_op jit(solution)/shard_map/gains/pallas_call | solution.py:263
  20.0 1.1 %all-to-all-done.refs_0_ = bf16[16,72,128]{2,1,0:T(8,128)(2,1)S(1)} async-done(((bf16[16,72,128]{2,1,0:T(8,128)(2,1)}), bf16[16,72,128]{2,1,0:T(8,128)(2,1)S(1)}, u32[]{:S(2)}, u32[]{:S(2)}) %all-to-all-start) | async-done | bytes 294944 | tf_op jit(solution)/shard_map/all_to_all | solution.py:255
  21.1 0.0 collective-permute-start
  21.1 1.6 %collective-permute-done.refs_1_ = bf16[16,72,128]{2,1,0:T(8,128)(2,1)S(1)} collective-permute-done((bf16[16,72,128]{2,1,0:T(8,128)(2,1)S(1)}, bf16[16,72,128]{2,1,0:T(8,128)(2,1)S(1)}, u32[]{:S(2)}, u32[]{:S(2)}) %collective-permute-start) | collective-permute-done | bytes 294944 | tf_op jit(solution)/shard_map/ppermute | solution.py:283
  22.7 0.0 copy-done.1
  22.7 0.0 copy-done
  22.7 6.0 %signal.2 = (bf16[4,256,256]{2,1,0:T(8,128)(2,1)}, bf16[2048,128]{1,0:T(8,128)(2,1)S(1)}) custom-call(bf16[16,72,128]{2,1,0:T(8,128)(2,1)S(1)} %all-to-all-done.refs_0_, bf16[16,72,128]{2,1,0:T(8,128)(2,1)S(1)} %collective-permute-done.refs_1_, s32[1]{0:T(128)} %bitcast.3.first_ref.refs_2_.refs_0_, s32[256,4,128]{2,1,0:T(4,128)S(1)} %copy-done, ...), custom_call_target="tpu_custom_call" | custom-call | flops 2147483648 | bytes 4194304 | tf_op jit(solution)/shard_map/signal/pallas_call | solution.py:300
  28.7 3.5 %all-to-all-start.1 = ((bf16[4,256,256]{2,1,0:T(8,128)(2,1)}), bf16[4,256,256]{2,1,0:T(8,128)(2,1)S(1)}, u32[]{:S(2)}, u32[]{:S(2)}) async-start(bf16[4,256,256]{2,1,0:T(8,128)(2,1)} %get-tuple-element.11), calls=%async_computation.1 | async-start | bytes 1048576 | tf_op jit(solution)/shard_map/all_to_all | solution.py:327
  32.2 5.5 %signal.3 = bf16[4,256,256]{2,1,0:T(8,128)(2,1)} custom-call(s32[1]{0:T(128)} %bitcast.3.first_ref.refs_2_.refs_0_, bf16[2048,128]{1,0:T(8,128)(2,1)S(1)} %get-tuple-element.12.refs_1_, s32[256,4,128]{2,1,0:T(4,128)S(1)} %copy-done, f32[256,4,128]{2,1,0:T(4,128)S(1)} %copy-done.1, bf16[2,2048,1024]{2,1,0:T(8,128)(2,1)} %gains.1.refs_5_.refs_4_), custom_call_target="tpu_custom_call" | custom-call | flops 2147483648 | bytes 4194304 | tf_op jit(solution)/shard_map/signal/pallas_call | solution.py:300
  37.7 3.0 %all-to-all-done.1 = bf16[4,256,256]{2,1,0:T(8,128)(2,1)S(1)} async-done(((bf16[4,256,256]{2,1,0:T(8,128)(2,1)}), bf16[4,256,256]{2,1,0:T(8,128)(2,1)S(1)}, u32[]{:S(2)}, u32[]{:S(2)}) %all-to-all-start.1) | async-done | bytes 524320 | tf_op jit(solution)/shard_map/all_to_all | solution.py:327
  40.8 3.5 %all-to-all-start.2 = ((bf16[4,256,256]{2,1,0:T(8,128)(2,1)}), bf16[4,256,256]{2,1,0:T(8,128)(2,1)S(1)}, u32[]{:S(2)}, u32[]{:S(2)}) async-start(bf16[4,256,256]{2,1,0:T(8,128)(2,1)} %signal.3), calls=%async_computation.2 | async-start | bytes 1048576 | tf_op jit(solution)/shard_map/all_to_all | solution.py:327
  44.3 0.1 reduce_sum.33
  44.3 7.6 %all-to-all-done.2 = bf16[4,256,256]{2,1,0:T(8,128)(2,1)S(1)} async-done(((bf16[4,256,256]{2,1,0:T(8,128)(2,1)}), bf16[4,256,256]{2,1,0:T(8,128)(2,1)S(1)}, u32[]{:S(2)}, u32[]{:S(2)}) %all-to-all-start.2) | async-done | bytes 524320 | tf_op jit(solution)/shard_map/all_to_all | solution.py:327
  52.0 0.1 reduce_sum.34
  52.1 13.3 %all_to_all.20 = bf16[8,2,32,256]{3,2,1,0:T(8,128)(2,1)S(1)} all-to-all(bf16[8,2,32,256]{3,2,1,0:T(8,128)(2,1)S(1)} %pad_maximum_fusion), channel_id=1, replica_groups={{0,1,8,9,16,17,24,25},{2,3,10,11,18,19,26,27},{4,5,12,13,20,21,28,29},{..., dimensions={0} | all-to-all | bytes 524288 | tf_op jit(solution)/shard_map/all_to_all | solution.py:333
  65.4 0.7 %copy.13 = f32[4,32,256]{2,0,1:T(4,128)} copy(f32[4,32,256]{2,1,0:T(8,128)S(1)} %bitcast.19) | data formatting | bytes 262144 | tf_op jit(solution)/shard_map/reshape | solution.py:342
  (2 shorter events, 0.1 us)
Async XLA Ops:
  0.0 22.7 %copy-start.1 = (f32[256,4,128]{2,1,0:T(4,128)S(1)}, f32[256,4,128]{2,1,0:T(4,128)}, u32[]{:S(2)}) copy-start(f32[256,4,128]{2,1,0:T(4,128)} %refs_3_.3) | copy-start | bytes 1572868
  0.0 22.7 %copy-start = (s32[256,4,128]{2,1,0:T(4,128)S(1)}, s32[256,4,128]{2,1,0:T(4,128)}, u32[]{:S(2)}) copy-start(s32[256,4,128]{2,1,0:T(4,128)} %refs_2_.1) | copy-start | bytes 1572868
  2.1 19.0 %all-to-all-start = ((bf16[16,72,128]{2,1,0:T(8,128)(2,1)}), bf16[16,72,128]{2,1,0:T(8,128)(2,1)S(1)}, u32[]{:S(2)}, u32[]{:S(2)}) async-start(bf16[16,72,128]{2,1,0:T(8,128)(2,1)} %pack.1), calls=%async_computation | async-start | bytes 589824 | tf_op jit(solution)/shard_map/all_to_all | solution.py:255
  21.1 1.6 %collective-permute-start = (bf16[16,72,128]{2,1,0:T(8,128)(2,1)S(1)}, bf16[16,72,128]{2,1,0:T(8,128)(2,1)S(1)}, u32[]{:S(2)}, u32[]{:S(2)}) collective-permute-start(bf16[16,72,128]{2,1,0:T(8,128)(2,1)S(1)} %all-to-all-done.refs_0_), channel_id=1, source_target_pairs={{0,1},{1,0},{2,3},{3,2},{4,5},{5,4},{6,7},{7,6},{8,9},{9,8},{10,11... | collective-permute-start | bytes 884744 | tf_op jit(solution)/shard_map/ppermute | solution.py:283
  28.7 12.1 %all-to-all-start.1 = ((bf16[4,256,256]{2,1,0:T(8,128)(2,1)}), bf16[4,256,256]{2,1,0:T(8,128)(2,1)S(1)}, u32[]{:S(2)}, u32[]{:S(2)}) async-start(bf16[4,256,256]{2,1,0:T(8,128)(2,1)} %get-tuple-element.11), calls=%async_computation.1 | async-start | bytes 1048576 | tf_op jit(solution)/shard_map/all_to_all | solution.py:327
  40.8 11.2 %all-to-all-start.2 = ((bf16[4,256,256]{2,1,0:T(8,128)(2,1)}), bf16[4,256,256]{2,1,0:T(8,128)(2,1)S(1)}, u32[]{:S(2)}, u32[]{:S(2)}) async-start(bf16[4,256,256]{2,1,0:T(8,128)(2,1)} %signal.3), calls=%async_computation.2 | async-start | bytes 1048576 | tf_op jit(solution)/shard_map/all_to_all | solution.py:327

commit v3 on v2

--- a/solution.py
+++ b/solution.py
@@ -157,20 +157,18 @@
     src[...] = held[...].astype(BF16)
 
 
-def signal_kernel(slots, terms, columns, lines, turn, *refs):
-    opening = turn == 0
-    if opening:
-        got_refs, refs = refs[:columns], refs[columns:]
-        block_ref, bin_ref, frac_ref, gain_ref, out_ref, src, held, arr, gains, turned, sem = refs
-    else:
-        block_ref, src, bin_ref, frac_ref, gain_ref, out_ref, arr, gains, turned, sem = refs
+def signal_kernel(slots, terms, columns, *refs):
+    got_refs, refs = refs[:columns], refs[columns:]
+    block_ref, bin_ref, frac_ref, gain_ref, out_ref, src, held, arr, gains, turned, sem = refs
     row_count, _, panels = bin_ref.shape
-    targets = out_ref.shape[0]
-    copy = pltpu.make_async_copy(gain_ref.at[turn], gains, sem)
-    copy.start()
-    if opening:
-        sum_rows(slots, terms, got_refs, held, src)
-    block = block_ref[0] + turn
+    planes, places, own, share, _ = out_ref.shape
+    copies = [
+        pltpu.make_async_copy(gain_ref.at[turn], gains.at[turn], sem.at[turn])
+        for turn in range(own)
+    ]
+    for copy in copies:
+        copy.start()
+    sum_rows(slots, terms, got_refs, held, src)
     half = 2 * terms
     upper = iota((half, panels), 0) < terms
     place = iota((half, panels), 0).astype(F32)
@@ -178,7 +176,7 @@
     def spread(value):
         return jnp.broadcast_to(value, (half, panels))
 
-    def weights(row):
+    def weights(block, row):
         here = bin_ref[row, pl.ds(block, 1), :].astype(F32)
         past = frac_ref[row, pl.ds(block, 1), :]
         tile = jnp.floor(here * (1.0 / half))
@@ -198,37 +196,46 @@
             before = match
         return jnp.concatenate(tiles, axis=0)
 
-    def step(index, carry):
-        for inner in range(PAIRS):
-            pair = index * PAIRS + inner
-            where = pl.ds(pl.multiple_of(pair * half, half), half)
-            rows16 = src[where, :]
-            zero = jnp.zeros_like(rows16)
-            lhs = jnp.concatenate(
-                [jnp.where(upper, rows16, zero), jnp.where(upper, zero, rows16)], axis=1
-            )
-            rhs = jnp.concatenate([weights(2 * pair), weights(2 * pair + 1)], axis=1)
-            if inner % 3 < 2:
-                turned[inner] = rhs.T
-                binned = jnp.dot(lhs, turned[inner], preferred_element_type=F32)
-            else:
-                binned = lax.dot_general(
-                    lhs, rhs, (((1,), (1,)), ((), ())), preferred_element_type=F32
+    def bin_rows(block):
+        def step(index, carry):
+            for inner in range(PAIRS):
+                pair = index * PAIRS + inner
+                where = pl.ds(pl.multiple_of(pair * half, half), half)
+                rows16 = src[where, :]
+                zero = jnp.zeros_like(rows16)
+                lhs = jnp.concatenate(
+                    [jnp.where(upper, rows16, zero), jnp.where(upper, zero, rows16)], axis=1
                 )
-            arr[where, :] = binned.astype(BF16)
+                rhs = jnp.concatenate(
+                    [weights(block, 2 * pair), weights(block, 2 * pair + 1)], axis=1
+                )
+                if inner % 3 < 2:
+                    turned[inner] = rhs.T
+                    binned = jnp.dot(lhs, turned[inner], preferred_element_type=F32)
+                else:
+                    binned = lax.dot_general(
+                        lhs, rhs, (((1,), (1,)), ((), ())), preferred_element_type=F32
+                    )
+                arr[where, :] = binned.astype(BF16)
+            return carry
+
+        lax.fori_loop(0, row_count // (2 * PAIRS), step, 0)
+
+    def block_step(turn, carry):
+        bin_rows(block_ref[0] + turn)
+        pltpu.make_async_copy(gain_ref.at[turn], gains.at[turn], sem.at[turn]).wait()
+        out_t = lax.dot_general(
+            arr[...], gains[turn], (((0,), (0,)), ((), ())), preferred_element_type=F32
+        )
+        out = out_t.T.astype(BF16)
+        for line in range(places // columns):
+            for plane in range(planes):
+                for column in range(columns):
+                    start = ((line * planes + plane) * columns + column) * share
+                    out_ref[plane, line * columns + column, turn] = out[start : start + share, :]
         return carry
 
-    lax.fori_loop(0, row_count // (2 * PAIRS), step, 0)
-    copy.wait()
-    out_t = lax.dot_general(
-        arr[...], gains[...], (((0,), (0,)), ((), ())), preferred_element_type=F32
-    )
-    out = out_t.T.astype(BF16)
-    piece = out.shape[0] // (targets * lines)
-    for line in range(lines):
-        for target in range(targets):
-            start = (line * targets + target) * piece
-            out_ref[target, line * piece : (line + 1) * piece, :] = out[start : start + piece, :]
+    lax.fori_loop(0, own, block_step, 0)
 
 
 def on_device(sources, owners, strip_rows, panel_counts, arrival_bins, arrival_fracs, gain_table):
@@ -283,62 +290,41 @@
             lax.ppermute(got, "gy", [(i, (i + turn) % columns) for i in range(columns)])
         )
     share = observers // devices
-    planes = 1
-    while planes * planes < shards:
-        planes *= 2
-    lines = shards // planes
+    planes, lines = shards, 1
     in_plane = [[line * planes + i for i in range(planes)] for line in range(lines)]
     in_line = [
         [(line * planes + i) * columns + j for line in range(lines) for j in range(columns)]
         for i in range(planes)
     ]
-    plane_sums, row_sources = [], None
-    for turn in range(own):
-        opening = turn == 0
-        partial = jax.ShapeDtypeStruct((planes, lines * columns * share, NBIN), BF16)
-        source = jax.ShapeDtypeStruct((rows_here * terms, panels), BF16)
-        made = pl.pallas_call(
-            functools.partial(signal_kernel, slots, terms, columns, lines, turn),
-            out_shape=(partial, source) if opening else (partial,),
-            in_specs=([VMEM] * columns + [SMEM] if opening else [SMEM, VMEM]) + [VMEM] * 2 + [HBM],
-            out_specs=(VMEM, VMEM) if opening else (VMEM,),
-            scratch_shapes=([pltpu.VMEM((rows_here * terms, panels), F32)] if opening else [])
-            + [
-                pltpu.VMEM((rows_here * terms, NBIN), BF16),
-                pltpu.VMEM((rows_here * terms, observers), BF16),
-                pltpu.VMEM((PAIRS, 2 * panels, NBIN), BF16),
-                pltpu.SemaphoreType.DMA,
-            ],
-            name="signal",
-            compiler_params=pltpu.CompilerParams(vmem_limit_bytes=48 << 20),
-            cost_estimate=pl.CostEstimate(
-                flops=2 * rows_here * terms * NBIN * (observers + panels * 8),
-                bytes_accessed=2 * rows_here * terms * observers,
-                transcendentals=0,
-            ),
-        )(
-            *(parts + [first.reshape(1)] if opening else [first.reshape(1), row_sources]),
-            arrival_bins,
-            arrival_fracs,
-            own_gains,
-        )
-        if opening:
-            row_sources = made[1]
-        met = lax.all_to_all(
-            made[0], "gx", split_axis=0, concat_axis=0, axis_index_groups=in_plane, tiled=True
-        )
-        plane_sums.append(
-            jnp.sum(met.astype(F32), axis=0).astype(BF16).reshape(lines * columns, share, NBIN)
-        )
+    partial = pl.pallas_call(
+        functools.partial(signal_kernel, slots, terms, columns),
+        out_shape=jax.ShapeDtypeStruct((planes, lines * columns, own, share, NBIN), BF16),
+        in_specs=[VMEM] * columns + [SMEM] + [VMEM] * 2 + [HBM],
+        out_specs=VMEM,
+        scratch_shapes=[
+            pltpu.VMEM((rows_here * terms, panels), BF16),
+            pltpu.VMEM((rows_here * terms, panels), F32),
+            pltpu.VMEM((rows_here * terms, NBIN), BF16),
+            pltpu.VMEM((own, rows_here * terms, observers), BF16),
+            pltpu.VMEM((PAIRS, 2 * panels, NBIN), BF16),
+            pltpu.SemaphoreType.DMA((own,)),
+        ],
+        name="signal",
+        compiler_params=pltpu.CompilerParams(vmem_limit_bytes=48 << 20),
+        cost_estimate=pl.CostEstimate(
+            flops=2 * own * rows_here * terms * NBIN * (observers + panels * 8),
+            bytes_accessed=2 * own * rows_here * terms * observers,
+            transcendentals=0,
+        ),
+    )(*parts, first.reshape(1), arrival_bins, arrival_fracs, own_gains)
     met = lax.all_to_all(
-        jnp.stack(plane_sums, axis=1),
+        partial.reshape(devices, own, share, NBIN),
         ("gx", "gy"),
         split_axis=0,
         concat_axis=0,
-        axis_index_groups=in_line,
         tiled=True,
     )
-    sums = jnp.sum(met.reshape(lines, columns, own, share, NBIN).astype(F32), axis=0)
+    sums = jnp.sum(met.reshape(shards, columns, own, share, NBIN).astype(F32), axis=0)
     return jnp.transpose(sums.reshape(blocks, share, NBIN), (1, 0, 2))
 
 

time: 66.6 us -> 64.6 us (0.970)
  blocking collectives: 13.3 us -> 31 us
  waiting for transfers between devices: 13.4 us -> 2.56 us
  starting transfers between devices: 15.3 us -> 8.35 us
  Pallas kernels: 23.2 us -> 21.5 us
    all_to_all x1, blocking collectives: 13.3 us -> 31 us  [on_device(): lax.all_to_all(partial.reshape(devices, own, share, NBIN), ('gx', 'gy'),...]
    all_to_all x2 -> x0, waiting for transfers between devices: 10.7 us -> none  [on_device(): lax.all_to_all(made[0], 'gx', split_axis=0, concat_axis=0, axis_index_gro...]
    all_to_all x2 -> x0, starting transfers between devices: 6.95 us -> none  [on_device(): lax.all_to_all(made[0], 'gx', split_axis=0, concat_axis=0, axis_index_gro...]
    pallas_call x2 -> x1, Pallas kernels: 11.6 us -> 9.85 us  [on_device(): pl.pallas_call(functools.partial(signal_kernel, slots, terms, columns), o...]
  transfers between devices with their start and end apart: 4 -> 2, of which waited for: 4 -> 2; matrix products, arithmetic and copies ran while one was open for 0% -> 0% of each run, Pallas kernels for 23% -> 15%
where the time goes in v3:
time: 64.6 us; the launch traced here: 64.4 us
  blocking collectives  31 us (48%)
  Pallas kernels  21.5 us (33%)
  starting transfers between devices  8.35 us (13%)
  waiting for transfers between devices  2.56 us (4%)
  local copies, waits for them, and re-layouts  0.75 us (1%)
    all_to_all x1, blocking collectives, on_device(): lax.all_to_all(partial.reshape(devices, own, share, NBIN), ('gx', 'gy'),...  31 us
    pallas_call x1, Pallas kernels, on_device(): pl.pallas_call(functools.partial(signal_kernel, slots, terms, columns), o...  9.85 us
    pallas_call x1, Pallas kernels, on_device(): pl.pallas_call(functools.partial(gains_kernel, blocks), out_shape=jax.Sha...  9.66 us
    all_to_all x1, starting transfers between devices, on_device(): got = lax.all_to_all(send, 'gx', split_axis=0, concat_axis=0, tiled=True)  8.34 us
    pallas_call x1, Pallas kernels, on_device(): pl.pallas_call(functools.partial(pack_kernel, slots), out_shape=jax.Shape...  1.96 us
    ppermute x1, waiting for transfers between devices, on_device(): lax.ppermute(got, 'gy', [(i, (i + turn) % columns) for i in range(columns)])  1.58 us
  transfers between devices with their start and end apart: 2, of which 2 were waited for; matrix products, arithmetic and copies ran while one was open for 0% of the time, Pallas kernels for 15%

profile of v3, /device:TPU:0, one launch (start us, length us, event | category | flops | bytes accessed | tf_op | source)
XLA Modules:
  0.0 64.4 jit_solution(11662528408660427591)
XLA Ops:
  0.0 2.0 %pack.1 = bf16[16,72,128]{2,1,0:T(8,128)(2,1)} custom-call(bf16[64,8,128]{2,1,0:T(8,128)(2,1)} %src_ref.1, s32[1,64]{1,0:T(1,128)} %bitcast.20, s32[1,64]{1,0:T(1,128)} %bitcast.21, s32[1,64]{1,0:T(1,128)} %bitcast.22), custom_call_target="tpu_custom_call" | custom-call | tf_op jit(solution)/shard_map/pack/pallas_call | solution.py:253
  2.0 8.3 %all-to-all-start = ((bf16[16,72,128]{2,1,0:T(8,128)(2,1)}), bf16[16,72,128]{2,1,0:T(8,128)(2,1)S(1)}, u32[]{:S(2)}, u32[]{:S(2)}) async-start(bf16[16,72,128]{2,1,0:T(8,128)(2,1)} %pack.1), calls=%async_computation | async-start | bytes 589824 | tf_op jit(solution)/shard_map/all_to_all | solution.py:262
  10.3 0.0 copy-start
  10.3 0.0 copy-start.1
  10.3 9.7 %gains.1.refs_5_ = bf16[2,2048,1024]{2,1,0:T(8,128)(2,1)} custom-call(s32[1]{0:T(128)} %bitcast.3.first_ref.refs_2_, bf16[65536,128]{1,0:T(8,128)(2,1)} %bitcast.17), custom_call_target="tpu_custom_call" | custom-call | flops 167772160 | bytes 25165824 | tf_op jit(solution)/shard_map/gains/pallas_call | solution.py:270
  20.0 1.0 %all-to-all-done.refs_0_ = bf16[16,72,128]{2,1,0:T(8,128)(2,1)S(1)} async-done(((bf16[16,72,128]{2,1,0:T(8,128)(2,1)}), bf16[16,72,128]{2,1,0:T(8,128)(2,1)S(1)}, u32[]{:S(2)}, u32[]{:S(2)}) %all-to-all-start) | async-done | bytes 294944 | tf_op jit(solution)/shard_map/all_to_all | solution.py:262
  21.0 0.0 collective-permute-start
  21.0 1.6 %collective-permute-done.refs_1_ = bf16[16,72,128]{2,1,0:T(8,128)(2,1)S(1)} collective-permute-done((bf16[16,72,128]{2,1,0:T(8,128)(2,1)S(1)}, bf16[16,72,128]{2,1,0:T(8,128)(2,1)S(1)}, u32[]{:S(2)}, u32[]{:S(2)}) %collective-permute-start) | collective-permute-done | bytes 294944 | tf_op jit(solution)/shard_map/ppermute | solution.py:290
  22.6 0.0 copy-done
  22.6 0.0 copy-done.1
  22.6 9.9 %signal.1 = bf16[16,2,2,32,256]{4,3,2,1,0:T(8,128)(2,1)S(1)} custom-call(bf16[16,72,128]{2,1,0:T(8,128)(2,1)S(1)} %all-to-all-done.refs_0_, bf16[16,72,128]{2,1,0:T(8,128)(2,1)S(1)} %collective-permute-done.refs_1_, s32[1]{0:T(128)} %bitcast.3.first_ref.refs_2_, s32[256,4,128]{2,1,0:T(4,128)S(1)} %copy-done, f32[256,4,128]{2,1,0:T(4,128)S(1)} %copy-done.1, ...), custom_call_target="tpu_custom_call" | custom-call | flops 4294967296 | bytes 8388608 | tf_op jit(solution)/shard_map/signal/pallas_call | solution.py:299
  32.4 31.0 %all_to_all.10 = bf16[32,2,32,256]{3,2,1,0:T(8,128)(2,1)S(1)} all-to-all(bf16[32,2,32,256]{3,2,1,0:T(8,128)(2,1)S(1)} %bitcast.16), channel_id=1, replica_groups=mesh['gx'=16,'gy'=2] {'gx','gy'}, dimensions={0} | all-to-all | bytes 2097152 | tf_op jit(solution)/shard_map/all_to_all | solution.py:320
  63.4 0.2 convert_reduce_fusion
  63.6 0.7 %copy.12 = f32[4,32,256]{2,0,1:T(4,128)} copy(f32[4,32,256]{2,1,0:T(8,128)S(1)} %bitcast.19) | data formatting | bytes 262144 | tf_op jit(solution)/shard_map/reshape | solution.py:328
Async XLA Ops:
  2.0 19.0 %all-to-all-start = ((bf16[16,72,128]{2,1,0:T(8,128)(2,1)}), bf16[16,72,128]{2,1,0:T(8,128)(2,1)S(1)}, u32[]{:S(2)}, u32[]{:S(2)}) async-start(bf16[16,72,128]{2,1,0:T(8,128)(2,1)} %pack.1), calls=%async_computation | async-start | bytes 589824 | tf_op jit(solution)/shard_map/all_to_all | solution.py:262
  10.3 12.3 %copy-start = (s32[256,4,128]{2,1,0:T(4,128)S(1)}, s32[256,4,128]{2,1,0:T(4,128)}, u32[]{:S(2)}) copy-start(s32[256,4,128]{2,1,0:T(4,128)} %refs_3_.1) | copy-start | bytes 1572868
  10.3 12.2 %copy-start.1 = (f32[256,4,128]{2,1,0:T(4,128)S(1)}, f32[256,4,128]{2,1,0:T(4,128)}, u32[]{:S(2)}) copy-start(f32[256,4,128]{2,1,0:T(4,128)} %refs_4_.1) | copy-start | bytes 1572868
  21.0 1.6 %collective-permute-start = (bf16[16,72,128]{2,1,0:T(8,128)(2,1)S(1)}, bf16[16,72,128]{2,1,0:T(8,128)(2,1)S(1)}, u32[]{:S(2)}, u32[]{:S(2)}) collective-permute-start(bf16[16,72,128]{2,1,0:T(8,128)(2,1)S(1)} %all-to-all-done.refs_0_), channel_id=1, source_target_pairs={{0,1},{1,0},{2,3},{3,2},{4,5},{5,4},{6,7},{7,6},{8,9},{9,8},{10,11... | collective-permute-start | bytes 884744 | tf_op jit(solution)/shard_map/ppermute | solution.py:290

commit v4 on v3

--- a/solution.py
+++ b/solution.py
@@ -10,8 +10,8 @@
 NBIN = 256
 LANES = 128
 STEP = 128
-DEPTH = 8
-SPARE = 4
+DEPTH = 12
+SPARE = 6
 F32 = jnp.float32
 BF16 = jnp.bfloat16
 VMEM = pl.BlockSpec(memory_space=pltpu.VMEM)
@@ -57,7 +57,7 @@
     )
 
 
-PAIRS = 64
+PAIRS = 128
 
 
 def gains_kernel(blocks, first_ref, view_ref, out_ref, inward, outward, in_sem, out_sem):

time: 64.6 us -> 64.2 us (level)
  no operation moved by 1% of the time
where the time goes in v4:
time: 64.2 us; the launch traced here: 63.9 us
  blocking collectives  30.9 us (48%)
  Pallas kernels  21 us (33%)
  starting transfers between devices  8.35 us (13%)
  waiting for transfers between devices  2.68 us (4%)
  local copies, waits for them, and re-layouts  0.75 us (1%)
    all_to_all x1, blocking collectives, on_device(): lax.all_to_all(partial.reshape(devices, own, share, NBIN), ('gx', 'gy'),...  30.9 us
    pallas_call x1, Pallas kernels, on_device(): pl.pallas_call(functools.partial(gains_kernel, blocks), out_shape=jax.Sha...  9.54 us
    pallas_call x1, Pallas kernels, on_device(): pl.pallas_call(functools.partial(signal_kernel, slots, terms, columns), o...  9.52 us
    all_to_all x1, starting transfers between devices, on_device(): got = lax.all_to_all(send, 'gx', split_axis=0, concat_axis=0, tiled=True)  8.34 us
    pallas_call x1, Pallas kernels, on_device(): pl.pallas_call(functools.partial(pack_kernel, slots), out_shape=jax.Shape...  1.96 us
    ppermute x1, waiting for transfers between devices, on_device(): lax.ppermute(got, 'gy', [(i, (i + turn) % columns) for i in range(columns)])  1.58 us
  transfers between devices with their start and end apart: 2, of which 2 were waited for; matrix products, arithmetic and copies ran while one was open for 0% of the time, Pallas kernels for 15%

profile of v4, /device:TPU:0, one launch (start us, length us, event | category | flops | bytes accessed | tf_op | source)
XLA Modules:
  0.0 63.9 jit_solution(4339599047770995393)
XLA Ops:
  0.0 2.0 %pack.1 = bf16[16,72,128]{2,1,0:T(8,128)(2,1)} custom-call(bf16[64,8,128]{2,1,0:T(8,128)(2,1)} %src_ref.1, s32[1,64]{1,0:T(1,128)} %bitcast.20, s32[1,64]{1,0:T(1,128)} %bitcast.21, s32[1,64]{1,0:T(1,128)} %bitcast.22), custom_call_target="tpu_custom_call" | custom-call | tf_op jit(solution)/shard_map/pack/pallas_call | solution.py:253
  2.0 8.3 %all-to-all-start = ((bf16[16,72,128]{2,1,0:T(8,128)(2,1)}), bf16[16,72,128]{2,1,0:T(8,128)(2,1)S(1)}, u32[]{:S(2)}, u32[]{:S(2)}) async-start(bf16[16,72,128]{2,1,0:T(8,128)(2,1)} %pack.1), calls=%async_computation | async-start | bytes 589824 | tf_op jit(solution)/shard_map/all_to_all | solution.py:262
  10.3 0.0 copy-start
  10.3 0.0 copy-start.1
  10.3 9.5 %gains.1.refs_5_ = bf16[2,2048,1024]{2,1,0:T(8,128)(2,1)} custom-call(s32[1]{0:T(128)} %bitcast.3.first_ref.refs_2_, bf16[65536,128]{1,0:T(8,128)(2,1)} %bitcast.17), custom_call_target="tpu_custom_call" | custom-call | flops 167772160 | bytes 25165824 | tf_op jit(solution)/shard_map/gains/pallas_call | solution.py:270
  19.9 1.1 %all-to-all-done.refs_0_ = bf16[16,72,128]{2,1,0:T(8,128)(2,1)S(1)} async-done(((bf16[16,72,128]{2,1,0:T(8,128)(2,1)}), bf16[16,72,128]{2,1,0:T(8,128)(2,1)S(1)}, u32[]{:S(2)}, u32[]{:S(2)}) %all-to-all-start) | async-done | bytes 294944 | tf_op jit(solution)/shard_map/all_to_all | solution.py:262
  21.0 0.0 collective-permute-start
  21.0 1.6 %collective-permute-done.refs_1_ = bf16[16,72,128]{2,1,0:T(8,128)(2,1)S(1)} collective-permute-done((bf16[16,72,128]{2,1,0:T(8,128)(2,1)S(1)}, bf16[16,72,128]{2,1,0:T(8,128)(2,1)S(1)}, u32[]{:S(2)}, u32[]{:S(2)}) %collective-permute-start) | collective-permute-done | bytes 294944 | tf_op jit(solution)/shard_map/ppermute | solution.py:290
  22.6 0.0 copy-done
  22.6 0.0 copy-done.1
  22.6 9.5 %signal.1 = bf16[16,2,2,32,256]{4,3,2,1,0:T(8,128)(2,1)S(1)} custom-call(bf16[16,72,128]{2,1,0:T(8,128)(2,1)S(1)} %all-to-all-done.refs_0_, bf16[16,72,128]{2,1,0:T(8,128)(2,1)S(1)} %collective-permute-done.refs_1_, s32[1]{0:T(128)} %bitcast.3.first_ref.refs_2_, s32[256,4,128]{2,1,0:T(4,128)S(1)} %copy-done, f32[256,4,128]{2,1,0:T(4,128)S(1)} %copy-done.1, ...), custom_call_target="tpu_custom_call" | custom-call | flops 4294967296 | bytes 8388608 | tf_op jit(solution)/shard_map/signal/pallas_call | solution.py:299
  32.1 30.9 %all_to_all.10 = bf16[32,2,32,256]{3,2,1,0:T(8,128)(2,1)S(1)} all-to-all(bf16[32,2,32,256]{3,2,1,0:T(8,128)(2,1)S(1)} %bitcast.16), channel_id=1, replica_groups=mesh['gx'=16,'gy'=2] {'gx','gy'}, dimensions={0} | all-to-all | bytes 2097152 | tf_op jit(solution)/shard_map/all_to_all | solution.py:320
  63.0 0.2 convert_reduce_fusion
  63.2 0.7 %copy.12 = f32[4,32,256]{2,0,1:T(4,128)} copy(f32[4,32,256]{2,1,0:T(8,128)S(1)} %bitcast.19) | data formatting | bytes 262144 | tf_op jit(solution)/shard_map/reshape | solution.py:328
Async XLA Ops:
  2.0 19.0 %all-to-all-start = ((bf16[16,72,128]{2,1,0:T(8,128)(2,1)}), bf16[16,72,128]{2,1,0:T(8,128)(2,1)S(1)}, u32[]{:S(2)}, u32[]{:S(2)}) async-start(bf16[16,72,128]{2,1,0:T(8,128)(2,1)} %pack.1), calls=%async_computation | async-start | bytes 589824 | tf_op jit(solution)/shard_map/all_to_all | solution.py:262
  10.3 12.3 %copy-start = (s32[256,4,128]{2,1,0:T(4,128)S(1)}, s32[256,4,128]{2,1,0:T(4,128)}, u32[]{:S(2)}) copy-start(s32[256,4,128]{2,1,0:T(4,128)} %refs_3_.1) | copy-start | bytes 1572868
  10.3 12.2 %copy-start.1 = (f32[256,4,128]{2,1,0:T(4,128)S(1)}, f32[256,4,128]{2,1,0:T(4,128)}, u32[]{:S(2)}) copy-start(f32[256,4,128]{2,1,0:T(4,128)} %refs_4_.1) | copy-start | bytes 1572868
  21.0 1.6 %collective-permute-start = (bf16[16,72,128]{2,1,0:T(8,128)(2,1)S(1)}, bf16[16,72,128]{2,1,0:T(8,128)(2,1)S(1)}, u32[]{:S(2)}, u32[]{:S(2)}) collective-permute-start(bf16[16,72,128]{2,1,0:T(8,128)(2,1)S(1)} %all-to-all-done.refs_0_), channel_id=1, source_target_pairs={{0,1},{1,0},{2,3},{3,2},{4,5},{5,4},{6,7},{7,6},{8,9},{9,8},{10,11... | collective-permute-start | bytes 884744 | tf_op jit(solution)/shard_map/ppermute | solution.py:290

commit v5 on v4

--- a/solution.py
+++ b/solution.py
@@ -196,7 +196,7 @@
             before = match
         return jnp.concatenate(tiles, axis=0)
 
-    def bin_rows(block):
+    def bin_rows(block, turn):
         def step(index, carry):
             for inner in range(PAIRS):
                 pair = index * PAIRS + inner
@@ -216,16 +216,18 @@
                     binned = lax.dot_general(
                         lhs, rhs, (((1,), (1,)), ((), ())), preferred_element_type=F32
                     )
-                arr[where, :] = binned.astype(BF16)
+                arr[turn, where, :] = binned.astype(BF16)
             return carry
 
-        lax.fori_loop(0, row_count // (2 * PAIRS), step, 0)
-
-    def block_step(turn, carry):
-        bin_rows(block_ref[0] + turn)
-        pltpu.make_async_copy(gain_ref.at[turn], gains.at[turn], sem.at[turn]).wait()
+        lax.fori_loop(0, row_count // (2 * PAIRS), step, 0, unroll=True)
+
+    def block_step(turn):
+        bin_rows(block_ref[0] + turn, turn)
+        if turn == 0:
+            for copy in copies:
+                copy.wait()
         out_t = lax.dot_general(
-            arr[...], gains[turn], (((0,), (0,)), ((), ())), preferred_element_type=F32
+            arr[turn], gains[turn], (((0,), (0,)), ((), ())), preferred_element_type=F32
         )
         out = out_t.T.astype(BF16)
         for line in range(places // columns):
@@ -233,9 +235,9 @@
                 for column in range(columns):
                     start = ((line * planes + plane) * columns + column) * share
                     out_ref[plane, line * columns + column, turn] = out[start : start + share, :]
-        return carry
-
-    lax.fori_loop(0, own, block_step, 0)
+
+    for turn in range(own):
+        block_step(turn)
 
 
 def on_device(sources, owners, strip_rows, panel_counts, arrival_bins, arrival_fracs, gain_table):
@@ -304,7 +306,7 @@
         scratch_shapes=[
             pltpu.VMEM((rows_here * terms, panels), BF16),
             pltpu.VMEM((rows_here * terms, panels), F32),
-            pltpu.VMEM((rows_here * terms, NBIN), BF16),
+            pltpu.VMEM((own, rows_here * terms, NBIN), BF16),
             pltpu.VMEM((own, rows_here * terms, observers), BF16),
             pltpu.VMEM((PAIRS, 2 * panels, NBIN), BF16),
             pltpu.SemaphoreType.DMA((own,)),

time: 64.2 us -> 63.7 us (level)
  no operation moved by 1% of the time
where the time goes in v5:
time: 63.7 us; the launch traced here: 63.5 us
  blocking collectives  30.9 us (49%)
  Pallas kernels  20.6 us (32%)
  starting transfers between devices  8.35 us (13%)
  waiting for transfers between devices  2.68 us (4%)
  local copies, waits for them, and re-layouts  0.75 us (1%)
    all_to_all x1, blocking collectives, on_device(): lax.all_to_all(partial.reshape(devices, own, share, NBIN), ('gx', 'gy'),...  30.9 us
    pallas_call x1, Pallas kernels, on_device(): pl.pallas_call(functools.partial(gains_kernel, blocks), out_shape=jax.Sha...  9.54 us
    pallas_call x1, Pallas kernels, on_device(): pl.pallas_call(functools.partial(signal_kernel, slots, terms, columns), o...  9.11 us
    all_to_all x1, starting transfers between devices, on_device(): got = lax.all_to_all(send, 'gx', split_axis=0, concat_axis=0, tiled=True)  8.34 us
    pallas_call x1, Pallas kernels, on_device(): pl.pallas_call(functools.partial(pack_kernel, slots), out_shape=jax.Shape...  1.96 us
    ppermute x1, waiting for transfers between devices, on_device(): lax.ppermute(got, 'gy', [(i, (i + turn) % columns) for i in range(columns)])  1.58 us
  transfers between devices with their start and end apart: 2, of which 2 were waited for; matrix products, arithmetic and copies ran while one was open for 0% of the time, Pallas kernels for 15%

profile of v5, /device:TPU:0, one launch (start us, length us, event | category | flops | bytes accessed | tf_op | source)
XLA Modules:
  0.0 63.5 jit_solution(11189745599886551482)
XLA Ops:
  0.0 2.0 %pack.1 = bf16[16,72,128]{2,1,0:T(8,128)(2,1)} custom-call(bf16[64,8,128]{2,1,0:T(8,128)(2,1)} %src_ref.1, s32[1,64]{1,0:T(1,128)} %bitcast.20, s32[1,64]{1,0:T(1,128)} %bitcast.21, s32[1,64]{1,0:T(1,128)} %bitcast.22), custom_call_target="tpu_custom_call" | custom-call | tf_op jit(solution)/shard_map/pack/pallas_call | solution.py:255
  2.0 8.3 %all-to-all-start = ((bf16[16,72,128]{2,1,0:T(8,128)(2,1)}), bf16[16,72,128]{2,1,0:T(8,128)(2,1)S(1)}, u32[]{:S(2)}, u32[]{:S(2)}) async-start(bf16[16,72,128]{2,1,0:T(8,128)(2,1)} %pack.1), calls=%async_computation | async-start | bytes 589824 | tf_op jit(solution)/shard_map/all_to_all | solution.py:264
  10.3 0.0 copy-start
  10.3 0.0 copy-start.1
  10.3 9.5 %gains.1.refs_5_ = bf16[2,2048,1024]{2,1,0:T(8,128)(2,1)} custom-call(s32[1]{0:T(128)} %bitcast.3.first_ref.refs_2_, bf16[65536,128]{1,0:T(8,128)(2,1)} %bitcast.17), custom_call_target="tpu_custom_call" | custom-call | flops 167772160 | bytes 25165824 | tf_op jit(solution)/shard_map/gains/pallas_call | solution.py:272
  19.9 1.1 %all-to-all-done.refs_0_ = bf16[16,72,128]{2,1,0:T(8,128)(2,1)S(1)} async-done(((bf16[16,72,128]{2,1,0:T(8,128)(2,1)}), bf16[16,72,128]{2,1,0:T(8,128)(2,1)S(1)}, u32[]{:S(2)}, u32[]{:S(2)}) %all-to-all-start) | async-done | bytes 294944 | tf_op jit(solution)/shard_map/all_to_all | solution.py:264
  21.0 0.0 collective-permute-start
  21.0 1.6 %collective-permute-done.refs_1_ = bf16[16,72,128]{2,1,0:T(8,128)(2,1)S(1)} collective-permute-done((bf16[16,72,128]{2,1,0:T(8,128)(2,1)S(1)}, bf16[16,72,128]{2,1,0:T(8,128)(2,1)S(1)}, u32[]{:S(2)}, u32[]{:S(2)}) %collective-permute-start) | collective-permute-done | bytes 294944 | tf_op jit(solution)/shard_map/ppermute | solution.py:292
  22.6 0.0 copy-done
  22.6 0.0 copy-done.1
  22.6 9.1 %signal.1 = bf16[16,2,2,32,256]{4,3,2,1,0:T(8,128)(2,1)S(1)} custom-call(bf16[16,72,128]{2,1,0:T(8,128)(2,1)S(1)} %all-to-all-done.refs_0_, bf16[16,72,128]{2,1,0:T(8,128)(2,1)S(1)} %collective-permute-done.refs_1_, s32[1]{0:T(128)} %bitcast.3.first_ref.refs_2_, s32[256,4,128]{2,1,0:T(4,128)S(1)} %copy-done, f32[256,4,128]{2,1,0:T(4,128)S(1)} %copy-done.1, ...), custom_call_target="tpu_custom_call" | custom-call | flops 4294967296 | bytes 8388608 | tf_op jit(solution)/shard_map/signal/pallas_call | solution.py:301
  31.7 30.9 %all_to_all.10 = bf16[32,2,32,256]{3,2,1,0:T(8,128)(2,1)S(1)} all-to-all(bf16[32,2,32,256]{3,2,1,0:T(8,128)(2,1)S(1)} %bitcast.16), channel_id=1, replica_groups=mesh['gx'=16,'gy'=2] {'gx','gy'}, dimensions={0} | all-to-all | bytes 2097152 | tf_op jit(solution)/shard_map/all_to_all | solution.py:322
  62.6 0.2 convert_reduce_fusion
  62.8 0.7 %copy.12 = f32[4,32,256]{2,0,1:T(4,128)} copy(f32[4,32,256]{2,1,0:T(8,128)S(1)} %bitcast.19) | data formatting | bytes 262144 | tf_op jit(solution)/shard_map/reshape | solution.py:330
Async XLA Ops:
  2.0 19.0 %all-to-all-start = ((bf16[16,72,128]{2,1,0:T(8,128)(2,1)}), bf16[16,72,128]{2,1,0:T(8,128)(2,1)S(1)}, u32[]{:S(2)}, u32[]{:S(2)}) async-start(bf16[16,72,128]{2,1,0:T(8,128)(2,1)} %pack.1), calls=%async_computation | async-start | bytes 589824 | tf_op jit(solution)/shard_map/all_to_all | solution.py:264
  10.3 12.3 %copy-start = (s32[256,4,128]{2,1,0:T(4,128)S(1)}, s32[256,4,128]{2,1,0:T(4,128)}, u32[]{:S(2)}) copy-start(s32[256,4,128]{2,1,0:T(4,128)} %refs_3_.1) | copy-start | bytes 1572868
  10.3 12.2 %copy-start.1 = (f32[256,4,128]{2,1,0:T(4,128)S(1)}, f32[256,4,128]{2,1,0:T(4,128)}, u32[]{:S(2)}) copy-start(f32[256,4,128]{2,1,0:T(4,128)} %refs_4_.1) | copy-start | bytes 1572868
  21.0 1.6 %collective-permute-start = (bf16[16,72,128]{2,1,0:T(8,128)(2,1)S(1)}, bf16[16,72,128]{2,1,0:T(8,128)(2,1)S(1)}, u32[]{:S(2)}, u32[]{:S(2)}) collective-permute-start(bf16[16,72,128]{2,1,0:T(8,128)(2,1)S(1)} %all-to-all-done.refs_0_), channel_id=1, source_target_pairs={{0,1},{1,0},{2,3},{3,2},{4,5},{5,4},{6,7},{7,6},{8,9},{9,8},{10,11... | collective-permute-start | bytes 884744 | tf_op jit(solution)/shard_map/ppermute | solution.py:292
